TPU v7x, 32 devices: a whole 2x2x4 slice. The times are simulated.
32 devices in a mesh: grp: 2 (over x), patch: 16 (over z, y, core).
Axes of the slice: x: 2, y: 2, z: 4, core: 2. Of those that a mesh axis runs over, the one named last changes fastest.
Arguments:
- features: bfloat16 [4, 16, 32, 640], P('grp', 'patch'), parts along dimension 0, may hold values from -6 to 6
- stale_conv_in: bfloat16 [4, 16, 32, 640], P('grp', 'patch'), parts along dimension 0, may hold values from -4.1875 to 4.1875
- stale_normed: bfloat16 [4, 16, 32, 640], P('grp', 'patch'), parts along dimension 0, may hold values from -6 to 6
- first_gain: float32 [640], replicated, may hold values from 0.1 to 1.9
- first_bias: float32 [640], replicated, may hold values from -1.8 to 1.8
- conv_weight: bfloat16 [3, 3, 640, 640], replicated, may hold values from -0.078125 to 0.078125
- conv_bias: float32 [640], replicated, may hold values from -1.8 to 1.8
- second_gain: float32 [640], replicated, may hold values from 0.1 to 1.9
- second_bias: float32 [640], replicated, may hold values from -1.8 to 1.8
- query_weight: bfloat16 [640, 640], replicated, may hold values from -6 to 6
- key_weight: bfloat16 [640, 640], replicated, may hold values from -6 to 6
- value_weight: bfloat16 [640, 640], replicated, may hold values from -0.25 to 0.25
- output_weight: bfloat16 [640, 640], replicated, may hold values from -0.25 to 0.25
- layer_gain: float32 [640], replicated, may hold values from 0.1 to 1.9
- cross_query: bfloat16 [640, 640], replicated, may hold values from -0.5 to 0.5
- cross_output: bfloat16 [640, 640], replicated, may hold values from -0.25 to 0.25
- text_keys: bfloat16 [4, 77, 640], P('grp'), parts along dimension 0, may hold values from -32 to 32
- text_values: bfloat16 [4, 77, 640], P('grp'), parts along dimension 0, may hold values from -6 to 6
Outputs:
- block_output: float32 [4, 16, 32, 640], P('grp', 'patch'), parts along dimension 0
There are 2 independent parts, one for each index of `grp`. A program takes and returns all parts, laid end to end along the dimension named above; an argument that names none is the same for every part. Nothing has to cross between parts.
All inputs are finite; a program needn't handle non-finite values.
Results may differ from a plain program's by a relative error of at most 0.02.
The roundings to bfloat16 on the way count: a program that leaves them out, or rounds other values in their place, can miss the bound.
Values may be sent and summed in bfloat16 or wider, within the bound.
No kernel may reach another device: no remote copies, remote signals or barrier semaphores. Data moves between devices by JAX's collectives and lax.ppermute only.
A program may use at most 128 MiB of HBM per device.

v0:
```python
import functools

import jax
import jax.numpy as jnp
from jax import lax
from jax.experimental import pallas as pl
from jax.experimental.pallas import tpu as pltpu
from jax.sharding import PartitionSpec as P

GROUPS = 32
HEADS = 10
HEAD_DIM = 64
EPSILON = 1e-05


VMEM = pl.BlockSpec(memory_space=pltpu.VMEM)
HBM = pl.BlockSpec(memory_space=pltpu.HBM)
F32 = jnp.float32
BF16 = jnp.bfloat16


def exchange(value, axis, apart):
    return lax.ppermute(value, axis, [(i, i ^ apart) for i in range(lax.axis_size(axis))])


def shifted(value, axis, steps):
    count = lax.axis_size(axis)
    initial, last = (max(0, -steps), min(count, count - steps))
    return lax.ppermute(value, axis, [(source, source + steps) for source in range(initial, last)])


def total_over(value, axis):
    apart = lax.axis_size(axis) // 2
    while True:
        other = exchange(value, axis, apart)
        if apart == 1:
            return value, other
        value = value + other
        apart //= 2


def dot(a, b):
    return jnp.dot(a, b, preferred_element_type=F32)


def per_channel(sums, count):
    channels = sums.shape[-1]
    width = channels // GROUPS
    channel = lax.broadcasted_iota(jnp.int32, (channels, GROUPS), 0)
    low = lax.broadcasted_iota(jnp.int32, (channels, GROUPS), 1) * width
    member = jnp.where((channel >= low) & (channel < low + width), 1.0, 0.0)
    channel = lax.broadcasted_iota(jnp.int32, (GROUPS, channels), 1)
    low = lax.broadcasted_iota(jnp.int32, (GROUPS, channels), 0) * width
    spread = jnp.where((channel >= low) & (channel < low + width), 1.0, 0.0)
    exact = lax.Precision.HIGHEST
    grouped = jnp.dot(sums, member, preferred_element_type=F32, precision=exact)
    return jnp.dot(grouped, spread, preferred_element_type=F32, precision=exact) / count


def normalised(x, moments, image, images, gain, bias):
    mean = moments[image : image + 1]
    var = moments[images + image : images + image + 1] - mean * mean
    return (x - mean) * lax.rsqrt(var + EPSILON) * gain + bias


def three_taps(x, left, right):
    row = lax.broadcasted_iota(jnp.int32, x.shape, 0)
    last = x.shape[0] - 1
    return (
        jnp.where(row == 0, left, pltpu.roll(x, 1, 0)),
        x,
        jnp.where(row == last, right, pltpu.roll(x, last, 0)),
    )


def conv_body(
    features_ref, mine_ref, other_ref, gain_ref, bias_ref, above_ref, level_ref, below_ref,
    conv_bias_ref, weight_ref, hidden_ref, sums_ref, weight_buf, sem, *, count,
):
    order = [(row, column) for row in (0, 2, 1) for column in range(3)]
    copies = [
        pltpu.make_async_copy(weight_ref.at[i, j], weight_buf.at[i, j], sem.at[3 * i + j])
        for i, j in order
    ]
    for copy in copies:
        copy.start()
    images = above_ref.shape[0]
    cells, channels = features_ref.shape
    columns = cells // images
    moments = per_channel(mine_ref[...] + other_ref[...], count)
    gain, bias, conv_bias = [r[...].reshape(1, channels) for r in (gain_ref, bias_ref, conv_bias_ref)]
    taps = {at: [] for at in order}
    for image in range(images):
        x = features_ref[image * columns : (image + 1) * columns].astype(F32)
        x = normalised(x, moments, image, images, gain, bias)
        fresh = x * jax.nn.sigmoid(x)
        for i, ref in enumerate((above_ref, level_ref, below_ref)):
            held = ref[image].astype(F32)
            middle = fresh if i == 1 else held[:columns]
            edges = (held[columns : columns + 1], held[columns + 1 : columns + 2])
            for j, tap in enumerate(three_taps(middle, *edges)):
                taps[i, j].append(tap)
    acc = features_ref[...].astype(F32) + conv_bias
    for copy, at in zip(copies, order):
        tap = jnp.concatenate(taps[at], axis=0).astype(BF16)
        copy.wait()
        acc = acc + dot(tap, weight_buf[at[0], at[1]])
    hidden_ref[...] = acc
    for image in range(images):
        x = acc[image * columns : (image + 1) * columns]
        sums_ref[image : image + 1] = jnp.sum(x, axis=0, keepdims=True)
        sums_ref[images + image : images + image + 1] = jnp.sum(x * x, axis=0, keepdims=True)


def conv(features, sums, gain, bias, above, level, below, conv_bias, conv_weight, count):
    cells, channels = features.shape
    return pl.pallas_call(
        functools.partial(conv_body, count=count),
        in_specs=[VMEM] * 9 + [HBM],
        out_specs=[VMEM, VMEM],
        out_shape=[
            jax.ShapeDtypeStruct((cells, channels), F32),
            jax.ShapeDtypeStruct(sums[0].shape, F32),
        ],
        scratch_shapes=[
            pltpu.VMEM(conv_weight.shape, BF16),
            pltpu.SemaphoreType.DMA((9,)),
        ],
        cost_estimate=pl.CostEstimate(
            flops=18 * cells * channels * channels,
            transcendentals=cells * channels,
            bytes_accessed=18 * channels * channels,
        ),
        name="conv",
    )(features, *sums, gain, bias, above, level, below, conv_bias, conv_weight)


def attention(queries, key_of, value_of):
    columns, _ = queries.shape
    parts = []
    for first in range(0, HEADS, 4):
        heads = min(4, HEADS - first)
        lanes = slice(first * HEAD_DIM, (first + heads) * HEAD_DIM)
        q = queries[:, lanes]
        lane = lax.broadcasted_iota(jnp.int32, q.shape, 1)
        inside = [(lane >= h * HEAD_DIM) & (lane < (h + 1) * HEAD_DIM) for h in range(heads)]
        stacked = jnp.concatenate([jnp.where(i, q, 0.0) for i in inside], axis=0).astype(BF16)
        scores = lax.dot_general(
            stacked, key_of(lanes), (((1,), (1,)), ((), ())), preferred_element_type=F32
        ) * (HEAD_DIM**-0.5)
        weights = jnp.exp(scores - jnp.max(scores, axis=-1, keepdims=True))
        total = jnp.sum(weights, axis=-1, keepdims=True)
        result = dot(weights.astype(BF16), value_of(lanes)) / total
        part = jnp.zeros_like(q)
        for h in range(heads):
            part = part + jnp.where(inside[h], result[h * columns : (h + 1) * columns], 0.0)
        parts.append(part)
    return jnp.concatenate(parts, axis=-1).astype(BF16)


def tail_body(
    hidden_ref, mine_ref, other_ref, gain_ref, bias_ref, layer_gain_ref, text_keys_ref, text_values_ref,
    near_keys_ref, far_keys_ref, near_values_ref, far_values_ref,
    wq_ref, wk_ref, wv_ref, wo_ref, cq_ref, co_ref,
    out_ref, keys_buf, values_buf, weights_buf, sem, *, count,
):
    near = near_keys_ref.shape[0]
    moves = [
        (wq_ref, weights_buf.at[0]),
        (wk_ref, weights_buf.at[1]),
        (wv_ref, weights_buf.at[2]),
        (near_keys_ref.at[pl.ds(1, near - 1)], keys_buf.at[pl.ds(1, near - 1)]),
        (far_keys_ref, keys_buf.at[pl.ds(near, near)]),
        (near_values_ref.at[pl.ds(1, near - 1)], values_buf.at[pl.ds(1, near - 1)]),
        (far_values_ref, values_buf.at[pl.ds(near, near)]),
        (wo_ref, weights_buf.at[3]),
        (cq_ref, weights_buf.at[4]),
        (co_ref, weights_buf.at[5]),
    ]
    copies = [pltpu.make_async_copy(a, b, sem.at[i]) for i, (a, b) in enumerate(moves)]
    for copy in copies:
        copy.start()
    cells, channels = hidden_ref.shape
    images = text_keys_ref.shape[0]
    columns = cells // images
    patches = 2 * near
    moments = per_channel(mine_ref[...] + other_ref[...], count)
    gain, bias, layer_gain = [r[...].reshape(1, channels) for r in (gain_ref, bias_ref, layer_gain_ref)]
    rows = [slice(image * columns, (image + 1) * columns) for image in range(images)]
    x = jnp.concatenate(
        [
            normalised(hidden_ref[rows[i]], moments, i, images, gain, bias)
            for i in range(images)
        ],
        axis=0,
    ).astype(BF16)
    copies[0].wait()
    queries = dot(x, weights_buf[0]).astype(BF16).astype(F32)
    copies[1].wait()
    keys = dot(x, weights_buf[1]).astype(BF16)
    copies[2].wait()
    values = dot(x, weights_buf[2]).astype(BF16)
    for image in range(images):
        keys_buf[0, image] = keys[rows[image]]
        values_buf[0, image] = values[rows[image]]
    for copy in copies[3:7]:
        copy.wait()
    own = []
    for image in range(images):
        flat = lambda buf, lanes: buf[:, image, :, lanes].reshape(
            patches * columns, lanes.stop - lanes.start
        )
        own.append(
            attention(queries[rows[image]], lambda l: flat(keys_buf, l), lambda l: flat(values_buf, l))
        )
    copies[7].wait()
    mixed = hidden_ref[...] + dot(jnp.concatenate(own, axis=0), weights_buf[3])
    centred = mixed - jnp.mean(mixed, axis=-1, keepdims=True)
    var = jnp.mean(centred * centred, axis=-1, keepdims=True)
    layer_in = (centred * lax.rsqrt(var + EPSILON) * layer_gain).astype(BF16)
    copies[8].wait()
    cross_q = dot(layer_in, weights_buf[4]).astype(BF16).astype(F32)
    crossed = [
        attention(
            cross_q[rows[image]],
            lambda l: text_keys_ref[image, :, l],
            lambda l: text_values_ref[image, :, l],
        )
        for image in range(images)
    ]
    copies[9].wait()
    out_ref[...] = mixed + dot(jnp.concatenate(crossed, axis=0), weights_buf[5])


def tail(hidden, sums, gain, bias, layer_gain, text_keys, text_values, kept, weights, count):
    cells, channels = hidden.shape
    near, images, columns, width = kept[0].shape
    buffer = pltpu.VMEM((2 * near, images, columns, width), BF16)
    return pl.pallas_call(
        functools.partial(tail_body, count=count),
        in_specs=[VMEM] * 8 + [HBM] * 10,
        out_specs=VMEM,
        out_shape=jax.ShapeDtypeStruct((cells, channels), F32),
        scratch_shapes=[
            buffer,
            buffer,
            pltpu.VMEM((6, channels, width), BF16),
            pltpu.SemaphoreType.DMA((10,)),
        ],
        cost_estimate=pl.CostEstimate(
            flops=12 * cells * channels * width + 16 * near * columns * cells * width,
            transcendentals=2 * near * columns * cells * HEADS,
            bytes_accessed=12 * channels * width + 8 * near * images * columns * width,
        ),
        name="tail",
    )(hidden, *sums, gain, bias, layer_gain, text_keys, text_values, *kept, *weights)


def on_device(
    features, stale_conv_in, stale_normed, first_gain, first_bias, conv_weight, conv_bias,
    second_gain, second_bias, query_weight, key_weight, value_weight, output_weight,
    layer_gain, cross_query, cross_output, text_keys, text_values,
):
    images, _, columns, channels = features.shape
    cells = images * columns
    patches = lax.axis_size("patch")
    count = patches * columns * (channels // GROUPS)
    wide = features.astype(F32)[:, 0]
    sums = jnp.concatenate([jnp.sum(wide, axis=1), jnp.sum(wide * wide, axis=1)], axis=0)
    sums = total_over(sums, "patch")

    stale = stale_conv_in[:, 0]
    right_side = lax.axis_index("patch") % 2 == 1
    across = exchange(stale, "patch", 1)
    left = jnp.where(right_side, across[:, -1:], 0)
    right = jnp.where(right_side, 0, across[:, :1])
    level = jnp.concatenate([stale, left, right, jnp.zeros_like(stale[:, :6])], axis=1)
    above = shifted(level, "patch", 2)
    below = shifted(level, "patch", -2)

    held = stale_normed.reshape(1, images, columns, channels)
    apart = patches // 2
    while apart:
        other = exchange(held, "patch", apart)
        if apart > 1:
            held = jnp.concatenate([held, other], axis=0)
        apart //= 2
    kept = []
    for weight in (key_weight, value_weight):
        for part in (held, other):
            kept.append(dot(part.reshape(-1, channels), weight).astype(BF16).reshape(part.shape))

    hidden, sums = conv(
        features.reshape(cells, channels), sums, first_gain, first_bias,
        above, level, below, conv_bias, conv_weight, count,
    )
    sums = total_over(sums, "patch")
    out = tail(
        hidden, sums, second_gain, second_bias, layer_gain, text_keys, text_values,
        kept, (query_weight, key_weight, value_weight, output_weight, cross_query, cross_output), count,
    )
    return out.reshape(images, 1, columns, channels)


def solution(mesh):
    split = P("grp", "patch", None, None)
    in_specs = (split,) * 3 + (P(),) * 13 + (P("grp", None, None),) * 2
    return jax.shard_map(on_device, mesh=mesh, in_specs=in_specs, out_specs=split, check_vma=False)
```

profile of v0, /device:TPU:0, one launch (start us, length us, event | category | flops | bytes accessed | tf_op | source)
XLA Modules:
  0.0 68.7 jit_solution(11867445008022469650)
XLA Ops:
  0.5 3.6 %collective-permute-start.11 = (bf16[1,2,32,640]{3,2,1,0:T(8,128)(2,1)}, bf16[1,2,32,640]{3,2,1,0:T(8,128)(2,1)S(1)}, u32[]{:S(2)}, u32[]{:S(2)}) collective-permute-start(bf16[1,2,32,640]{3,2,1,0:T(8,128)(2,1)} %bitcast.20), channel_id=1, source_target_pairs={{0,8},{1,9},{2,10},{3,11},{4,12},{5,13},{6,14},{7,15},{8,0},{9,1},... | collective-permute-start | bytes 245768 | tf_op jit(solution)/shard_map/ppermute | solution.py:23
  5.3 4.0 %collective-permute-done.11 = bf16[1,2,32,640]{3,2,1,0:T(8,128)(2,1)S(1)} collective-permute-done((bf16[1,2,32,640]{3,2,1,0:T(8,128)(2,1)}, bf16[1,2,32,640]{3,2,1,0:T(8,128)(2,1)S(1)}, u32[]{:S(2)}, u32[]{:S(2)}) %collective-permute-start.11) | collective-permute-done | bytes 81952 | tf_op jit(solution)/shard_map/ppermute | solution.py:23
  10.2 1.0 %collective-permute-start.12 = (bf16[2,2,32,640]{3,2,1,0:T(8,128)(2,1)S(1)}, bf16[2,2,32,640]{3,2,1,0:T(8,128)(2,1)S(1)}, u32[]{:S(2)}, u32[]{:S(2)}) collective-permute-start(bf16[2,2,32,640]{3,2,1,0:T(8,128)(2,1)S(1)} %pad_maximum_fusion.2), channel_id=1, source_target_pairs={{0,4},{1,5},{2,6},{3,7},{4,0},{5,1},{6,2},{7,3},{8,12},{9,13},{10,... | collective-permute-start | bytes 491528 | tf_op jit(solution)/shard_map/ppermute | solution.py:23
  11.2 1.1 %collective-permute-start.1 = (f32[4,640]{1,0:T(4,128)S(1)}, f32[4,640]{1,0:T(4,128)S(1)}, u32[]{:S(2)}, u32[]{:S(2)}) collective-permute-start(f32[4,640]{1,0:T(4,128)S(1)} %fusion.1), channel_id=1, source_target_pairs={{0,4},{1,5},{2,6},{3,7},{4,0},{5,1},{6,2},{7,3},{8,12},{9,13},{10,... | collective-permute-start | bytes 30728 | tf_op jit(solution)/shard_map/ppermute | solution.py:23
  12.3 3.9 %collective-permute-done.12 = bf16[2,2,32,640]{3,2,1,0:T(8,128)(2,1)S(1)} collective-permute-done((bf16[2,2,32,640]{3,2,1,0:T(8,128)(2,1)S(1)}, bf16[2,2,32,640]{3,2,1,0:T(8,128)(2,1)S(1)}, u32[]{:S(2)}, u32[]{:S(2)}) %collective-permute-start.12) | collective-permute-done | bytes 163872 | tf_op jit(solution)/shard_map/ppermute | solution.py:23
  17.1 1.4 %collective-permute-start.13 = (bf16[4,2,32,640]{3,2,1,0:T(8,128)(2,1)S(1)}, bf16[4,2,32,640]{3,2,1,0:T(8,128)(2,1)S(1)}, u32[]{:S(2)}, u32[]{:S(2)}) collective-permute-start(bf16[4,2,32,640]{3,2,1,0:T(8,128)(2,1)S(1)} %pad_maximum_fusion.1), channel_id=1, source_target_pairs={{0,2},{1,3},{2,0},{3,1},{4,6},{5,7},{6,4},{7,5},{8,10},{9,11},{10,... | collective-permute-start | bytes 983048 | tf_op jit(solution)/shard_map/ppermute | solution.py:23
  18.5 1.0 %maximum_maximum_fusion.level_ref = bf16[2,40,640]{2,1,0:T(8,128)(2,1)S(1)} fusion(bf16[2,1,640]{2,1,0:T(2,128)(2,1)S(1)} %get-tuple-element.12, bf16[2,1,640]{2,1,0:T(2,128)(2,1)S(1)} %get-tuple-element.11, bf16[2,32,640]{2,1,0:T(8,128)(2,1)} %bitcast.32, bf16[40]{0:T(256)(128)(2,1)S(1)} %pad.12.clone), kind=kLoop, calls=%fused_computation.10 | loop fusion | flops 409600 | bytes 189520 | tf_op jit(solution)/shard_map/concatenate | solution.py:277
  19.5 2.6 %collective-permute-start.5 = (bf16[2,40,640]{2,1,0:T(8,128)(2,1)S(1)}, bf16[2,40,640]{2,1,0:T(8,128)(2,1)S(1)}, u32[]{:S(2)}, u32[]{:S(2)}) collective-permute-start(bf16[2,40,640]{2,1,0:T(8,128)(2,1)S(1)} %maximum_maximum_fusion.level_ref), channel_id=1, source_target_pairs={{0,2},{1,3},{2,4},{3,5},{4,6},{5,7},{6,8},{7,9},{8,10},{9,11},{10,... | collective-permute-start | bytes 307208 | tf_op jit(solution)/shard_map/ppermute | solution.py:29
  22.2 1.3 %collective-permute-start.6 = (bf16[2,40,640]{2,1,0:T(8,128)(2,1)S(1)}, bf16[2,40,640]{2,1,0:T(8,128)(2,1)S(1)}, u32[]{:S(2)}, u32[]{:S(2)}) collective-permute-start(bf16[2,40,640]{2,1,0:T(8,128)(2,1)S(1)} %maximum_maximum_fusion.level_ref), channel_id=1, source_target_pairs={{2,0},{3,1},{4,2},{5,3},{6,4},{7,5},{8,6},{9,7},{10,8},{11,9},{12,... | collective-permute-start | bytes 307208 | tf_op jit(solution)/shard_map/ppermute | solution.py:29
  23.5 2.1 %collective-permute-done.13 = bf16[4,2,32,640]{3,2,1,0:T(8,128)(2,1)S(1)} collective-permute-done((bf16[4,2,32,640]{3,2,1,0:T(8,128)(2,1)S(1)}, bf16[4,2,32,640]{3,2,1,0:T(8,128)(2,1)S(1)}, u32[]{:S(2)}, u32[]{:S(2)}) %collective-permute-start.13) | collective-permute-done | bytes 327712 | tf_op jit(solution)/shard_map/ppermute | solution.py:23
  25.8 2.2 %collective-permute-start.2 = (f32[4,640]{1,0:T(4,128)S(1)}, f32[4,640]{1,0:T(4,128)S(1)}, u32[]{:S(2)}, u32[]{:S(2)}) collective-permute-start(f32[4,640]{1,0:T(4,128)S(1)} %add.23), channel_id=1, source_target_pairs={{0,2},{1,3},{2,0},{3,1},{4,6},{5,7},{6,4},{7,5},{8,10},{9,11},{10,... | collective-permute-start | bytes 30728 | tf_op jit(solution)/shard_map/ppermute | solution.py:23
  28.0 1.7 %collective-permute-done.2 = f32[4,640]{1,0:T(4,128)S(1)} collective-permute-done((f32[4,640]{1,0:T(4,128)S(1)}, f32[4,640]{1,0:T(4,128)S(1)}, u32[]{:S(2)}, u32[]{:S(2)}) %collective-permute-start.2) | collective-permute-done | bytes 10272 | tf_op jit(solution)/shard_map/ppermute | solution.py:23
  29.7 1.2 %collective-permute-done.3.other_ref = f32[4,640]{1,0:T(4,128)S(1)} collective-permute-done((f32[4,640]{1,0:T(4,128)S(1)}, f32[4,640]{1,0:T(4,128)S(1)}, u32[]{:S(2)}, u32[]{:S(2)}) %collective-permute-start.3) | collective-permute-done | bytes 10272 | tf_op jit(solution)/shard_map/ppermute | solution.py:23
  31.5 5.5 %conv.1 = (f32[64,640]{1,0:T(8,128)}, f32[4,640]{1,0:T(4,128)}) custom-call(bf16[64,640]{1,0:T(8,128)(2,1)} %bitcast.30, f32[4,640]{1,0:T(4,128)} %copy-done.9, f32[4,640]{1,0:T(4,128)} %copy-done.11, f32[640]{0:T(1024)} %gain_ref.2, f32[640]{0:T(1024)} %bias_ref.2, bf16[2,40,640]{2,1,0:T(8,128)(2,1)} %copy-done.6, bf16[2,40,640]{2,1,0:T(8,128)(2,1)} %copy-done.3, ...), custom_call_target="tpu_custom_call" | custom-call | flops 471859200 | bytes 7372800 | tf_op jit(solution)/shard_map/conv/pallas_call | solution.py:117
  37.0 6.6 %collective-permute-start.7 = (f32[4,640]{1,0:T(4,128)}, f32[4,640]{1,0:T(4,128)S(1)}, u32[]{:S(2)}, u32[]{:S(2)}) collective-permute-start(f32[4,640]{1,0:T(4,128)} %get-tuple-element.8), channel_id=1, source_target_pairs={{0,8},{1,9},{2,10},{3,11},{4,12},{5,13},{6,14},{7,15},{8,0},{9,1},... | collective-permute-start | bytes 30728 | tf_op jit(solution)/shard_map/ppermute | solution.py:23
  43.6 1.9 %collective-permute-done.7 = f32[4,640]{1,0:T(4,128)S(1)} collective-permute-done((f32[4,640]{1,0:T(4,128)}, f32[4,640]{1,0:T(4,128)S(1)}, u32[]{:S(2)}, u32[]{:S(2)}) %collective-permute-start.7) | collective-permute-done | bytes 10272 | tf_op jit(solution)/shard_map/ppermute | solution.py:23
  46.2 1.5 %collective-permute-start.8 = (f32[4,640]{1,0:T(4,128)S(1)}, f32[4,640]{1,0:T(4,128)S(1)}, u32[]{:S(2)}, u32[]{:S(2)}) collective-permute-start(f32[4,640]{1,0:T(4,128)S(1)} %add.26), channel_id=1, source_target_pairs={{0,4},{1,5},{2,6},{3,7},{4,0},{5,1},{6,2},{7,3},{8,12},{9,13},{10,... | collective-permute-start | bytes 30728 | tf_op jit(solution)/shard_map/ppermute | solution.py:23
  47.6 2.2 %collective-permute-done.8 = f32[4,640]{1,0:T(4,128)S(1)} collective-permute-done((f32[4,640]{1,0:T(4,128)S(1)}, f32[4,640]{1,0:T(4,128)S(1)}, u32[]{:S(2)}, u32[]{:S(2)}) %collective-permute-start.8) | collective-permute-done | bytes 10272 | tf_op jit(solution)/shard_map/ppermute | solution.py:23
  51.3 2.2 %collective-permute-done.9 = f32[4,640]{1,0:T(4,128)S(1)} collective-permute-done((f32[4,640]{1,0:T(4,128)S(1)}, f32[4,640]{1,0:T(4,128)S(1)}, u32[]{:S(2)}, u32[]{:S(2)}) %collective-permute-start.9) | collective-permute-done | bytes 10272 | tf_op jit(solution)/shard_map/ppermute | solution.py:23
  53.5 1.6 %convolution_convert_fusion.3 = bf16[512,640]{1,0:T(8,128)(2,1)} fusion(bf16[512,640]{1,0:T(8,128)(2,1)S(1)} %bitcast.28, bf16[640,640]{1,0:T(8,128)(2,1)S(1)} %copy-done), kind=kOutput, calls=%fused_computation.3 | convolution fusion | flops 419758080 | bytes 2129920 | tf_op jit(solution)/shard_map/dot_general | solution.py:43
  55.2 1.6 %convolution_convert_fusion.1 = bf16[512,640]{1,0:T(8,128)(2,1)} fusion(bf16[512,640]{1,0:T(8,128)(2,1)S(1)} %bitcast.29, bf16[640,640]{1,0:T(8,128)(2,1)S(1)} %copy-done.1), kind=kOutput, calls=%fused_computation.1 | convolution fusion | flops 419758080 | bytes 2129920 | tf_op jit(solution)/shard_map/dot_general | solution.py:43
  56.8 1.6 %convolution_convert_fusion.2 = bf16[512,640]{1,0:T(8,128)(2,1)} fusion(bf16[512,640]{1,0:T(8,128)(2,1)S(1)} %bitcast.33, bf16[640,640]{1,0:T(8,128)(2,1)S(1)} %copy-done), kind=kOutput, calls=%fused_computation.2 | convolution fusion | flops 419758080 | bytes 2129920 | tf_op jit(solution)/shard_map/dot_general | solution.py:43
  58.4 1.6 %convolution_convert_fusion = bf16[512,640]{1,0:T(8,128)(2,1)} fusion(bf16[512,640]{1,0:T(8,128)(2,1)S(1)} %bitcast.34, bf16[640,640]{1,0:T(8,128)(2,1)S(1)} %copy-done.1), kind=kOutput, calls=%fused_computation | convolution fusion | flops 419758080 | bytes 2129920 | tf_op jit(solution)/shard_map/dot_general | solution.py:43
  60.6 8.1 %tail.1 = f32[64,640]{1,0:T(8,128)} custom-call(f32[64,640]{1,0:T(8,128)} %get-tuple-element.7.hidden_ref, f32[4,640]{1,0:T(4,128)} %copy-done.8, f32[4,640]{1,0:T(4,128)} %copy-done.10, f32[640]{0:T(1024)} %gain_ref.3, f32[640]{0:T(1024)} %bias_ref.3, f32[640]{0:T(1024)} %layer_gain_ref.1, bf16[2,77,640]{2,1,0:T(8,128)(2,1)} %copy.19.text_keys_ref, ...), custom_call_target="tpu_custom_call" | custom-call | flops 482344960 | bytes 7536640 | tf_op jit(solution)/shard_map/tail/pallas_call | solution.py:239
  (53 shorter events, 7.1 us)
Async XLA Ops:
  0.0 25.6 %copy-start.2 = (bf16[2,1,32,640]{3,2,1,0:T(8,128)(2,1)S(1)}, bf16[2,1,32,640]{3,2,1,0:T(8,128)(2,1)}, u32[]{:S(2)}) copy-start(bf16[2,1,32,640]{3,2,1,0:T(8,128)(2,1)} %param.20) | copy-start | bytes 245764
  0.0 18.5 %collective-permute-start.4 = (bf16[2,32,640]{2,1,0:T(8,128)(2,1)}, bf16[2,32,640]{2,1,0:T(8,128)(2,1)S(1)}, u32[]{:S(2)}, u32[]{:S(2)}) collective-permute-start(bf16[2,32,640]{2,1,0:T(8,128)(2,1)} %bitcast.31), channel_id=1, source_target_pairs={{0,1},{1,0},{2,3},{3,2},{4,5},{5,4},{6,7},{7,6},{8,9},{9,8},{10,11... | collective-permute-start | bytes 245768 | tf_op jit(solution)/shard_map/ppermute | solution.py:23
  0.5 8.8 %collective-permute-start.11 = (bf16[1,2,32,640]{3,2,1,0:T(8,128)(2,1)}, bf16[1,2,32,640]{3,2,1,0:T(8,128)(2,1)S(1)}, u32[]{:S(2)}, u32[]{:S(2)}) collective-permute-start(bf16[1,2,32,640]{3,2,1,0:T(8,128)(2,1)} %bitcast.20), channel_id=1, source_target_pairs={{0,8},{1,9},{2,10},{3,11},{4,12},{5,13},{6,14},{7,15},{8,0},{9,1},... | collective-permute-start | bytes 245768 | tf_op jit(solution)/shard_map/ppermute | solution.py:23
  5.1 6.1 %collective-permute-start = (f32[4,640]{1,0:T(4,128)S(1)}, f32[4,640]{1,0:T(4,128)S(1)}, u32[]{:S(2)}, u32[]{:S(2)}) collective-permute-start(f32[4,640]{1,0:T(4,128)S(1)} %pad_maximum_fusion.3), channel_id=1, source_target_pairs={{0,8},{1,9},{2,10},{3,11},{4,12},{5,13},{6,14},{7,15},{8,0},{9,1},... | collective-permute-start | bytes 30728 | tf_op jit(solution)/shard_map/ppermute | solution.py:23
  10.2 6.0 %collective-permute-start.12 = (bf16[2,2,32,640]{3,2,1,0:T(8,128)(2,1)S(1)}, bf16[2,2,32,640]{3,2,1,0:T(8,128)(2,1)S(1)}, u32[]{:S(2)}, u32[]{:S(2)}) collective-permute-start(bf16[2,2,32,640]{3,2,1,0:T(8,128)(2,1)S(1)} %pad_maximum_fusion.2), channel_id=1, source_target_pairs={{0,4},{1,5},{2,6},{3,7},{4,0},{5,1},{6,2},{7,3},{8,12},{9,13},{10,... | collective-permute-start | bytes 491528 | tf_op jit(solution)/shard_map/ppermute | solution.py:23
  11.2 14.5 %collective-permute-start.1 = (f32[4,640]{1,0:T(4,128)S(1)}, f32[4,640]{1,0:T(4,128)S(1)}, u32[]{:S(2)}, u32[]{:S(2)}) collective-permute-start(f32[4,640]{1,0:T(4,128)S(1)} %fusion.1), channel_id=1, source_target_pairs={{0,4},{1,5},{2,6},{3,7},{4,0},{5,1},{6,2},{7,3},{8,12},{9,13},{10,... | collective-permute-start | bytes 30728 | tf_op jit(solution)/shard_map/ppermute | solution.py:23
  17.1 8.5 %collective-permute-start.13 = (bf16[4,2,32,640]{3,2,1,0:T(8,128)(2,1)S(1)}, bf16[4,2,32,640]{3,2,1,0:T(8,128)(2,1)S(1)}, u32[]{:S(2)}, u32[]{:S(2)}) collective-permute-start(bf16[4,2,32,640]{3,2,1,0:T(8,128)(2,1)S(1)} %pad_maximum_fusion.1), channel_id=1, source_target_pairs={{0,2},{1,3},{2,0},{3,1},{4,6},{5,7},{6,4},{7,5},{8,10},{9,11},{10,... | collective-permute-start | bytes 983048 | tf_op jit(solution)/shard_map/ppermute | solution.py:23
  19.5 11.3 %copy-start.3 = (bf16[2,40,640]{2,1,0:T(8,128)(2,1)}, bf16[2,40,640]{2,1,0:T(8,128)(2,1)S(1)}, u32[]{:S(2)}) copy-start(bf16[2,40,640]{2,1,0:T(8,128)(2,1)S(1)} %maximum_maximum_fusion.level_ref) | copy-start | bytes 307204
  19.5 11.3 %collective-permute-start.5 = (bf16[2,40,640]{2,1,0:T(8,128)(2,1)S(1)}, bf16[2,40,640]{2,1,0:T(8,128)(2,1)S(1)}, u32[]{:S(2)}, u32[]{:S(2)}) collective-permute-start(bf16[2,40,640]{2,1,0:T(8,128)(2,1)S(1)} %maximum_maximum_fusion.level_ref), channel_id=1, source_target_pairs={{0,2},{1,3},{2,4},{3,5},{4,6},{5,7},{6,8},{7,9},{8,10},{9,11},{10,... | collective-permute-start | bytes 307208 | tf_op jit(solution)/shard_map/ppermute | solution.py:29
  22.2 8.7 %collective-permute-start.6 = (bf16[2,40,640]{2,1,0:T(8,128)(2,1)S(1)}, bf16[2,40,640]{2,1,0:T(8,128)(2,1)S(1)}, u32[]{:S(2)}, u32[]{:S(2)}) collective-permute-start(bf16[2,40,640]{2,1,0:T(8,128)(2,1)S(1)} %maximum_maximum_fusion.level_ref), channel_id=1, source_target_pairs={{2,0},{3,1},{4,2},{5,3},{6,4},{7,5},{8,6},{9,7},{10,8},{11,9},{12,... | collective-permute-start | bytes 307208 | tf_op jit(solution)/shard_map/ppermute | solution.py:29
  25.7 31.1 %collective-permute-start.14 = (bf16[8,2,32,640]{3,2,1,0:T(8,128)(2,1)S(1)}, bf16[8,2,32,640]{3,2,1,0:T(8,128)(2,1)S(1)}, u32[]{:S(2)}, u32[]{:S(2)}) collective-permute-start(bf16[8,2,32,640]{3,2,1,0:T(8,128)(2,1)S(1)} %pad_maximum_fusion), channel_id=1, source_target_pairs={{0,1},{1,0},{2,3},{3,2},{4,5},{5,4},{6,7},{7,6},{8,9},{9,8},{10,11... | collective-permute-start | bytes 1966088 | tf_op jit(solution)/shard_map/ppermute | solution.py:23
  25.8 3.8 %collective-permute-start.2 = (f32[4,640]{1,0:T(4,128)S(1)}, f32[4,640]{1,0:T(4,128)S(1)}, u32[]{:S(2)}, u32[]{:S(2)}) collective-permute-start(f32[4,640]{1,0:T(4,128)S(1)} %add.23), channel_id=1, source_target_pairs={{0,2},{1,3},{2,0},{3,1},{4,6},{5,7},{6,4},{7,5},{8,10},{9,11},{10,... | collective-permute-start | bytes 30728 | tf_op jit(solution)/shard_map/ppermute | solution.py:23
  29.6 1.2 %copy-start.9 = (f32[4,640]{1,0:T(4,128)}, f32[4,640]{1,0:T(4,128)S(1)}, u32[]{:S(2)}) copy-start(f32[4,640]{1,0:T(4,128)S(1)} %add.24.mine_ref) | copy-start | bytes 30724
  29.6 1.2 %collective-permute-start.3 = (f32[4,640]{1,0:T(4,128)S(1)}, f32[4,640]{1,0:T(4,128)S(1)}, u32[]{:S(2)}, u32[]{:S(2)}) collective-permute-start(f32[4,640]{1,0:T(4,128)S(1)} %add.24.mine_ref), channel_id=1, source_target_pairs={{0,1},{1,0},{2,3},{3,2},{4,5},{5,4},{6,7},{7,6},{8,9},{9,8},{10,11... | collective-permute-start | bytes 30728 | tf_op jit(solution)/shard_map/ppermute | solution.py:23
  30.8 0.7 copy-start.7
  31.5 18.3 %copy-start.4 = (bf16[2,77,640]{2,0,1:T(2,128)(2,1)S(1)}, bf16[2,77,640]{2,0,1:T(2,128)(2,1)}, u32[]{:S(2)}) copy-start(bf16[2,77,640]{2,0,1:T(2,128)(2,1)} %param.34) | copy-start | bytes 591364
  31.5 19.1 %copy-start.5 = (bf16[2,77,640]{2,0,1:T(2,128)(2,1)S(1)}, bf16[2,77,640]{2,0,1:T(2,128)(2,1)}, u32[]{:S(2)}) copy-start(bf16[2,77,640]{2,0,1:T(2,128)(2,1)} %param.35) | copy-start | bytes 591364
  31.5 22.0 %copy-start = (bf16[640,640]{1,0:T(8,128)(2,1)S(1)}, bf16[640,640]{1,0:T(8,128)(2,1)}, u32[]{:S(2)}) copy-start(bf16[640,640]{1,0:T(8,128)(2,1)} %wk_ref.1) | copy-start | bytes 2457604
  37.0 8.5 %collective-permute-start.7 = (f32[4,640]{1,0:T(4,128)}, f32[4,640]{1,0:T(4,128)S(1)}, u32[]{:S(2)}, u32[]{:S(2)}) collective-permute-start(f32[4,640]{1,0:T(4,128)} %get-tuple-element.8), channel_id=1, source_target_pairs={{0,8},{1,9},{2,10},{3,11},{4,12},{5,13},{6,14},{7,15},{8,0},{9,1},... | collective-permute-start | bytes 30728 | tf_op jit(solution)/shard_map/ppermute | solution.py:23
  46.2 3.7 %collective-permute-start.8 = (f32[4,640]{1,0:T(4,128)S(1)}, f32[4,640]{1,0:T(4,128)S(1)}, u32[]{:S(2)}, u32[]{:S(2)}) collective-permute-start(f32[4,640]{1,0:T(4,128)S(1)} %add.26), channel_id=1, source_target_pairs={{0,4},{1,5},{2,6},{3,7},{4,0},{5,1},{6,2},{7,3},{8,12},{9,13},{10,... | collective-permute-start | bytes 30728 | tf_op jit(solution)/shard_map/ppermute | solution.py:23
  49.8 3.7 %collective-permute-start.9 = (f32[4,640]{1,0:T(4,128)S(1)}, f32[4,640]{1,0:T(4,128)S(1)}, u32[]{:S(2)}, u32[]{:S(2)}) collective-permute-start(f32[4,640]{1,0:T(4,128)S(1)} %add.27), channel_id=1, source_target_pairs={{0,2},{1,3},{2,0},{3,1},{4,6},{5,7},{6,4},{7,5},{8,10},{9,11},{10,... | collective-permute-start | bytes 30728 | tf_op jit(solution)/shard_map/ppermute | solution.py:23
  51.3 3.9 %copy-start.1 = (bf16[640,640]{1,0:T(8,128)(2,1)S(1)}, bf16[640,640]{1,0:T(8,128)(2,1)}, u32[]{:S(2)}) copy-start(bf16[640,640]{1,0:T(8,128)(2,1)} %wv_ref.1) | copy-start | bytes 2457604
  53.5 3.3 %copy-start.8 = (f32[4,640]{1,0:T(4,128)}, f32[4,640]{1,0:T(4,128)S(1)}, u32[]{:S(2)}) copy-start(f32[4,640]{1,0:T(4,128)S(1)} %add.28.mine_ref) | copy-start | bytes 30724
  53.5 6.5 %collective-permute-start.10 = (f32[4,640]{1,0:T(4,128)S(1)}, f32[4,640]{1,0:T(4,128)S(1)}, u32[]{:S(2)}, u32[]{:S(2)}) collective-permute-start(f32[4,640]{1,0:T(4,128)S(1)} %add.28.mine_ref), channel_id=1, source_target_pairs={{0,1},{1,0},{2,3},{3,2},{4,5},{5,4},{6,7},{7,6},{8,9},{9,8},{10,11... | collective-permute-start | bytes 30728 | tf_op jit(solution)/shard_map/ppermute | solution.py:23
  (3 other events, 1.8 us)
where the time goes:
time: 69.1 us; the launch traced here: 68.7 us
  starting transfers between devices  22 us (32%)
  waiting for transfers between devices  19.1 us (28%)
  Pallas kernels  13.6 us (20%)
  matrix products  6.44 us (9%)
  other arithmetic  4.6 us (7%)
  local copies, waits for them, and re-layouts  2.76 us (4%)
    ppermute x13, waiting for transfers between devices, exchange(): lax.ppermute(value, axis, [(i, i ^ apart) for i in range(lax.axis_size(ax...  19.1 us
    ppermute x13, starting transfers between devices, exchange(): lax.ppermute(value, axis, [(i, i ^ apart) for i in range(lax.axis_size(ax...  18.1 us
    pallas_call x1, Pallas kernels, tail(): pl.pallas_call(functools.partial(tail_body, count=count), in_specs=[VMEM]...  8.09 us
    dot_general x4, matrix products, dot(): return jnp.dot(a, b, preferred_element_type=F32)  6.44 us
    pallas_call x1, Pallas kernels, conv(): pl.pallas_call(functools.partial(conv_body, count=count), in_specs=[VMEM]...  5.48 us
    ppermute x2, starting transfers between devices, shifted(): lax.ppermute(value, axis, [(source, source + steps) for source in range(i...  3.93 us
    unnamed x26, local copies, waits for them, and re-layouts  2.68 us
    concatenate x3, other arithmetic, on_device(): held = jnp.concatenate([held, other], axis=0)  1.92 us
  transfers between devices with their start and end apart: 15, of which 8 were waited for; matrix products, arithmetic and copies ran while one was open for 18% of the time, Pallas kernels for 8%

commit v1 on v0

--- a/solution.py
+++ b/solution.py
@@ -48,13 +48,19 @@
     width = channels // GROUPS
     channel = lax.broadcasted_iota(jnp.int32, (channels, GROUPS), 0)
     low = lax.broadcasted_iota(jnp.int32, (channels, GROUPS), 1) * width
-    member = jnp.where((channel >= low) & (channel < low + width), 1.0, 0.0)
+    member = jnp.where((channel >= low) & (channel < low + width), 1.0, 0.0).astype(BF16)
     channel = lax.broadcasted_iota(jnp.int32, (GROUPS, channels), 1)
     low = lax.broadcasted_iota(jnp.int32, (GROUPS, channels), 0) * width
-    spread = jnp.where((channel >= low) & (channel < low + width), 1.0, 0.0)
-    exact = lax.Precision.HIGHEST
-    grouped = jnp.dot(sums, member, preferred_element_type=F32, precision=exact)
-    return jnp.dot(grouped, spread, preferred_element_type=F32, precision=exact) / count
+    spread = jnp.where((channel >= low) & (channel < low + width), 1.0, 0.0).astype(BF16)
+    return exact_dot(exact_dot(sums, member), spread) / count
+
+
+def exact_dot(a, ones):
+    high = a.astype(BF16)
+    rest = a - high.astype(F32)
+    middle = rest.astype(BF16)
+    low = (rest - middle.astype(F32)).astype(BF16)
+    return dot(high, ones) + dot(middle, ones) + dot(low, ones)
 
 
 def normalised(x, moments, image, images, gain, bias):
@@ -77,11 +83,8 @@
     features_ref, mine_ref, other_ref, gain_ref, bias_ref, above_ref, level_ref, below_ref,
     conv_bias_ref, weight_ref, hidden_ref, sums_ref, weight_buf, sem, *, count,
 ):
-    order = [(row, column) for row in (0, 2, 1) for column in range(3)]
-    copies = [
-        pltpu.make_async_copy(weight_ref.at[i, j], weight_buf.at[i, j], sem.at[3 * i + j])
-        for i, j in order
-    ]
+    order = (0, 2, 1)
+    copies = [pltpu.make_async_copy(weight_ref.at[i], weight_buf.at[i], sem.at[i]) for i in order]
     for copy in copies:
         copy.start()
     images = above_ref.shape[0]
@@ -89,7 +92,7 @@
     columns = cells // images
     moments = per_channel(mine_ref[...] + other_ref[...], count)
     gain, bias, conv_bias = [r[...].reshape(1, channels) for r in (gain_ref, bias_ref, conv_bias_ref)]
-    taps = {at: [] for at in order}
+    taps = ([], [], [])
     for image in range(images):
         x = features_ref[image * columns : (image + 1) * columns].astype(F32)
         x = normalised(x, moments, image, images, gain, bias)
@@ -98,13 +101,13 @@
             held = ref[image].astype(F32)
             middle = fresh if i == 1 else held[:columns]
             edges = (held[columns : columns + 1], held[columns + 1 : columns + 2])
-            for j, tap in enumerate(three_taps(middle, *edges)):
-                taps[i, j].append(tap)
+            row_taps = three_taps(middle, *edges)
+            taps[i].append(jnp.concatenate([t.astype(BF16) for t in row_taps], axis=1))
     acc = features_ref[...].astype(F32) + conv_bias
-    for copy, at in zip(copies, order):
-        tap = jnp.concatenate(taps[at], axis=0).astype(BF16)
+    for i, copy in zip(order, copies):
         copy.wait()
-        acc = acc + dot(tap, weight_buf[at[0], at[1]])
+        tap = jnp.concatenate(taps[i], axis=0)
+        acc = acc + dot(tap, weight_buf[i].reshape(3 * channels, channels))
     hidden_ref[...] = acc
     for image in range(images):
         x = acc[image * columns : (image + 1) * columns]
@@ -124,7 +127,7 @@
         ],
         scratch_shapes=[
             pltpu.VMEM(conv_weight.shape, BF16),
-            pltpu.SemaphoreType.DMA((9,)),
+            pltpu.SemaphoreType.DMA((3,)),
         ],
         cost_estimate=pl.CostEstimate(
             flops=18 * cells * channels * channels,

time: 69.1 us -> 69.2 us (level)
  no operation moved by 1% of the time
where the time goes in v1:
time: 69.2 us; the launch traced here: 68.8 us
  starting transfers between devices  22 us (32%)
  waiting for transfers between devices  19.1 us (28%)
  Pallas kernels  13.7 us (20%)
  matrix products  6.45 us (9%)
  other arithmetic  4.6 us (7%)
  local copies, waits for them, and re-layouts  2.76 us (4%)
    ppermute x13, waiting for transfers between devices, exchange(): lax.ppermute(value, axis, [(i, i ^ apart) for i in range(lax.axis_size(ax...  19.1 us
    ppermute x13, starting transfers between devices, exchange(): lax.ppermute(value, axis, [(i, i ^ apart) for i in range(lax.axis_size(ax...  18.1 us
    pallas_call x1, Pallas kernels, tail(): pl.pallas_call(functools.partial(tail_body, count=count), in_specs=[VMEM]...  8.09 us
    dot_general x4, matrix products, dot(): return jnp.dot(a, b, preferred_element_type=F32)  6.45 us
    pallas_call x1, Pallas kernels, conv(): pl.pallas_call(functools.partial(conv_body, count=count), in_specs=[VMEM]...  5.63 us
    ppermute x2, starting transfers between devices, shifted(): lax.ppermute(value, axis, [(source, source + steps) for source in range(i...  3.93 us
    unnamed x26, local copies, waits for them, and re-layouts  2.68 us
    concatenate x3, other arithmetic, on_device(): held = jnp.concatenate([held, other], axis=0)  1.92 us
  transfers between devices with their start and end apart: 15, of which 8 were waited for; matrix products, arithmetic and copies ran while one was open for 18% of the time, Pallas kernels for 8%

profile of v1, /device:TPU:0, one launch (start us, length us, event | category | flops | bytes accessed | tf_op | source)
XLA Modules:
  0.0 68.8 jit_solution(11111826940124264197)
XLA Ops:
  0.5 3.6 %collective-permute-start.11 = (bf16[1,2,32,640]{3,2,1,0:T(8,128)(2,1)}, bf16[1,2,32,640]{3,2,1,0:T(8,128)(2,1)S(1)}, u32[]{:S(2)}, u32[]{:S(2)}) collective-permute-start(bf16[1,2,32,640]{3,2,1,0:T(8,128)(2,1)} %bitcast.20), channel_id=1, source_target_pairs={{0,8},{1,9},{2,10},{3,11},{4,12},{5,13},{6,14},{7,15},{8,0},{9,1},... | collective-permute-start | bytes 245768 | tf_op jit(solution)/shard_map/ppermute | solution.py:23
  5.3 4.0 %collective-permute-done.11 = bf16[1,2,32,640]{3,2,1,0:T(8,128)(2,1)S(1)} collective-permute-done((bf16[1,2,32,640]{3,2,1,0:T(8,128)(2,1)}, bf16[1,2,32,640]{3,2,1,0:T(8,128)(2,1)S(1)}, u32[]{:S(2)}, u32[]{:S(2)}) %collective-permute-start.11) | collective-permute-done | bytes 81952 | tf_op jit(solution)/shard_map/ppermute | solution.py:23
  10.2 1.0 %collective-permute-start.12 = (bf16[2,2,32,640]{3,2,1,0:T(8,128)(2,1)S(1)}, bf16[2,2,32,640]{3,2,1,0:T(8,128)(2,1)S(1)}, u32[]{:S(2)}, u32[]{:S(2)}) collective-permute-start(bf16[2,2,32,640]{3,2,1,0:T(8,128)(2,1)S(1)} %pad_maximum_fusion.2), channel_id=1, source_target_pairs={{0,4},{1,5},{2,6},{3,7},{4,0},{5,1},{6,2},{7,3},{8,12},{9,13},{10,... | collective-permute-start | bytes 491528 | tf_op jit(solution)/shard_map/ppermute | solution.py:23
  11.2 1.1 %collective-permute-start.1 = (f32[4,640]{1,0:T(4,128)S(1)}, f32[4,640]{1,0:T(4,128)S(1)}, u32[]{:S(2)}, u32[]{:S(2)}) collective-permute-start(f32[4,640]{1,0:T(4,128)S(1)} %fusion.1), channel_id=1, source_target_pairs={{0,4},{1,5},{2,6},{3,7},{4,0},{5,1},{6,2},{7,3},{8,12},{9,13},{10,... | collective-permute-start | bytes 30728 | tf_op jit(solution)/shard_map/ppermute | solution.py:23
  12.3 3.9 %collective-permute-done.12 = bf16[2,2,32,640]{3,2,1,0:T(8,128)(2,1)S(1)} collective-permute-done((bf16[2,2,32,640]{3,2,1,0:T(8,128)(2,1)S(1)}, bf16[2,2,32,640]{3,2,1,0:T(8,128)(2,1)S(1)}, u32[]{:S(2)}, u32[]{:S(2)}) %collective-permute-start.12) | collective-permute-done | bytes 163872 | tf_op jit(solution)/shard_map/ppermute | solution.py:23
  17.1 1.4 %collective-permute-start.13 = (bf16[4,2,32,640]{3,2,1,0:T(8,128)(2,1)S(1)}, bf16[4,2,32,640]{3,2,1,0:T(8,128)(2,1)S(1)}, u32[]{:S(2)}, u32[]{:S(2)}) collective-permute-start(bf16[4,2,32,640]{3,2,1,0:T(8,128)(2,1)S(1)} %pad_maximum_fusion.1), channel_id=1, source_target_pairs={{0,2},{1,3},{2,0},{3,1},{4,6},{5,7},{6,4},{7,5},{8,10},{9,11},{10,... | collective-permute-start | bytes 983048 | tf_op jit(solution)/shard_map/ppermute | solution.py:23
  18.5 1.0 %maximum_maximum_fusion.level_ref = bf16[2,40,640]{2,1,0:T(8,128)(2,1)S(1)} fusion(bf16[2,1,640]{2,1,0:T(2,128)(2,1)S(1)} %get-tuple-element.12, bf16[2,1,640]{2,1,0:T(2,128)(2,1)S(1)} %get-tuple-element.11, bf16[2,32,640]{2,1,0:T(8,128)(2,1)} %bitcast.32, bf16[40]{0:T(256)(128)(2,1)S(1)} %pad.12.clone), kind=kLoop, calls=%fused_computation.10 | loop fusion | flops 409600 | bytes 189520 | tf_op jit(solution)/shard_map/concatenate | solution.py:280
  19.5 2.6 %collective-permute-start.5 = (bf16[2,40,640]{2,1,0:T(8,128)(2,1)S(1)}, bf16[2,40,640]{2,1,0:T(8,128)(2,1)S(1)}, u32[]{:S(2)}, u32[]{:S(2)}) collective-permute-start(bf16[2,40,640]{2,1,0:T(8,128)(2,1)S(1)} %maximum_maximum_fusion.level_ref), channel_id=1, source_target_pairs={{0,2},{1,3},{2,4},{3,5},{4,6},{5,7},{6,8},{7,9},{8,10},{9,11},{10,... | collective-permute-start | bytes 307208 | tf_op jit(solution)/shard_map/ppermute | solution.py:29
  22.2 1.3 %collective-permute-start.6 = (bf16[2,40,640]{2,1,0:T(8,128)(2,1)S(1)}, bf16[2,40,640]{2,1,0:T(8,128)(2,1)S(1)}, u32[]{:S(2)}, u32[]{:S(2)}) collective-permute-start(bf16[2,40,640]{2,1,0:T(8,128)(2,1)S(1)} %maximum_maximum_fusion.level_ref), channel_id=1, source_target_pairs={{2,0},{3,1},{4,2},{5,3},{6,4},{7,5},{8,6},{9,7},{10,8},{11,9},{12,... | collective-permute-start | bytes 307208 | tf_op jit(solution)/shard_map/ppermute | solution.py:29
  23.5 2.1 %collective-permute-done.13 = bf16[4,2,32,640]{3,2,1,0:T(8,128)(2,1)S(1)} collective-permute-done((bf16[4,2,32,640]{3,2,1,0:T(8,128)(2,1)S(1)}, bf16[4,2,32,640]{3,2,1,0:T(8,128)(2,1)S(1)}, u32[]{:S(2)}, u32[]{:S(2)}) %collective-permute-start.13) | collective-permute-done | bytes 327712 | tf_op jit(solution)/shard_map/ppermute | solution.py:23
  25.8 2.2 %collective-permute-start.2 = (f32[4,640]{1,0:T(4,128)S(1)}, f32[4,640]{1,0:T(4,128)S(1)}, u32[]{:S(2)}, u32[]{:S(2)}) collective-permute-start(f32[4,640]{1,0:T(4,128)S(1)} %add.23), channel_id=1, source_target_pairs={{0,2},{1,3},{2,0},{3,1},{4,6},{5,7},{6,4},{7,5},{8,10},{9,11},{10,... | collective-permute-start | bytes 30728 | tf_op jit(solution)/shard_map/ppermute | solution.py:23
  28.0 1.7 %collective-permute-done.2 = f32[4,640]{1,0:T(4,128)S(1)} collective-permute-done((f32[4,640]{1,0:T(4,128)S(1)}, f32[4,640]{1,0:T(4,128)S(1)}, u32[]{:S(2)}, u32[]{:S(2)}) %collective-permute-start.2) | collective-permute-done | bytes 10272 | tf_op jit(solution)/shard_map/ppermute | solution.py:23
  29.7 1.2 %collective-permute-done.3.other_ref = f32[4,640]{1,0:T(4,128)S(1)} collective-permute-done((f32[4,640]{1,0:T(4,128)S(1)}, f32[4,640]{1,0:T(4,128)S(1)}, u32[]{:S(2)}, u32[]{:S(2)}) %collective-permute-start.3) | collective-permute-done | bytes 10272 | tf_op jit(solution)/shard_map/ppermute | solution.py:23
  31.5 5.6 %conv.1 = (f32[64,640]{1,0:T(8,128)}, f32[4,640]{1,0:T(4,128)}) custom-call(bf16[64,640]{1,0:T(8,128)(2,1)} %bitcast.30, f32[4,640]{1,0:T(4,128)} %copy-done.9, f32[4,640]{1,0:T(4,128)} %copy-done.11, f32[640]{0:T(1024)} %gain_ref.2, f32[640]{0:T(1024)} %bias_ref.2, bf16[2,40,640]{2,1,0:T(8,128)(2,1)} %copy-done.6, bf16[2,40,640]{2,1,0:T(8,128)(2,1)} %copy-done.3, ...), custom_call_target="tpu_custom_call" | custom-call | flops 471859200 | bytes 7372800 | tf_op jit(solution)/shard_map/conv/pallas_call | solution.py:120
  37.1 6.6 %collective-permute-start.7 = (f32[4,640]{1,0:T(4,128)}, f32[4,640]{1,0:T(4,128)S(1)}, u32[]{:S(2)}, u32[]{:S(2)}) collective-permute-start(f32[4,640]{1,0:T(4,128)} %get-tuple-element.8), channel_id=1, source_target_pairs={{0,8},{1,9},{2,10},{3,11},{4,12},{5,13},{6,14},{7,15},{8,0},{9,1},... | collective-permute-start | bytes 30728 | tf_op jit(solution)/shard_map/ppermute | solution.py:23
  43.7 1.9 %collective-permute-done.7 = f32[4,640]{1,0:T(4,128)S(1)} collective-permute-done((f32[4,640]{1,0:T(4,128)}, f32[4,640]{1,0:T(4,128)S(1)}, u32[]{:S(2)}, u32[]{:S(2)}) %collective-permute-start.7) | collective-permute-done | bytes 10272 | tf_op jit(solution)/shard_map/ppermute | solution.py:23
  46.3 1.5 %collective-permute-start.8 = (f32[4,640]{1,0:T(4,128)S(1)}, f32[4,640]{1,0:T(4,128)S(1)}, u32[]{:S(2)}, u32[]{:S(2)}) collective-permute-start(f32[4,640]{1,0:T(4,128)S(1)} %add.26), channel_id=1, source_target_pairs={{0,4},{1,5},{2,6},{3,7},{4,0},{5,1},{6,2},{7,3},{8,12},{9,13},{10,... | collective-permute-start | bytes 30728 | tf_op jit(solution)/shard_map/ppermute | solution.py:23
  47.8 2.2 %collective-permute-done.8 = f32[4,640]{1,0:T(4,128)S(1)} collective-permute-done((f32[4,640]{1,0:T(4,128)S(1)}, f32[4,640]{1,0:T(4,128)S(1)}, u32[]{:S(2)}, u32[]{:S(2)}) %collective-permute-start.8) | collective-permute-done | bytes 10272 | tf_op jit(solution)/shard_map/ppermute | solution.py:23
  51.4 2.2 %collective-permute-done.9 = f32[4,640]{1,0:T(4,128)S(1)} collective-permute-done((f32[4,640]{1,0:T(4,128)S(1)}, f32[4,640]{1,0:T(4,128)S(1)}, u32[]{:S(2)}, u32[]{:S(2)}) %collective-permute-start.9) | collective-permute-done | bytes 10272 | tf_op jit(solution)/shard_map/ppermute | solution.py:23
  53.7 1.6 %convolution_convert_fusion.3 = bf16[512,640]{1,0:T(8,128)(2,1)} fusion(bf16[512,640]{1,0:T(8,128)(2,1)S(1)} %bitcast.28, bf16[640,640]{1,0:T(8,128)(2,1)S(1)} %copy-done), kind=kOutput, calls=%fused_computation.3 | convolution fusion | flops 419758080 | bytes 2129920 | tf_op jit(solution)/shard_map/dot_general | solution.py:43
  55.3 1.6 %convolution_convert_fusion.1 = bf16[512,640]{1,0:T(8,128)(2,1)} fusion(bf16[512,640]{1,0:T(8,128)(2,1)S(1)} %bitcast.29, bf16[640,640]{1,0:T(8,128)(2,1)S(1)} %copy-done.1), kind=kOutput, calls=%fused_computation.1 | convolution fusion | flops 419758080 | bytes 2129920 | tf_op jit(solution)/shard_map/dot_general | solution.py:43
  56.9 1.6 %convolution_convert_fusion.2 = bf16[512,640]{1,0:T(8,128)(2,1)} fusion(bf16[512,640]{1,0:T(8,128)(2,1)S(1)} %bitcast.33, bf16[640,640]{1,0:T(8,128)(2,1)S(1)} %copy-done), kind=kOutput, calls=%fused_computation.2 | convolution fusion | flops 419758080 | bytes 2129920 | tf_op jit(solution)/shard_map/dot_general | solution.py:43
  58.5 1.6 %convolution_convert_fusion = bf16[512,640]{1,0:T(8,128)(2,1)} fusion(bf16[512,640]{1,0:T(8,128)(2,1)S(1)} %bitcast.34, bf16[640,640]{1,0:T(8,128)(2,1)S(1)} %copy-done.1), kind=kOutput, calls=%fused_computation | convolution fusion | flops 419758080 | bytes 2129920 | tf_op jit(solution)/shard_map/dot_general | solution.py:43
  60.7 8.1 %tail.1 = f32[64,640]{1,0:T(8,128)} custom-call(f32[64,640]{1,0:T(8,128)} %get-tuple-element.7.hidden_ref, f32[4,640]{1,0:T(4,128)} %copy-done.8, f32[4,640]{1,0:T(4,128)} %copy-done.10, f32[640]{0:T(1024)} %gain_ref.3, f32[640]{0:T(1024)} %bias_ref.3, f32[640]{0:T(1024)} %layer_gain_ref.1, bf16[2,77,640]{2,1,0:T(8,128)(2,1)} %copy.19.text_keys_ref, ...), custom_call_target="tpu_custom_call" | custom-call | flops 482344960 | bytes 7536640 | tf_op jit(solution)/shard_map/tail/pallas_call | solution.py:242
  (53 shorter events, 7.1 us)
Async XLA Ops:
  0.0 25.6 %copy-start.2 = (bf16[2,1,32,640]{3,2,1,0:T(8,128)(2,1)S(1)}, bf16[2,1,32,640]{3,2,1,0:T(8,128)(2,1)}, u32[]{:S(2)}) copy-start(bf16[2,1,32,640]{3,2,1,0:T(8,128)(2,1)} %param.20) | copy-start | bytes 245764
  0.0 18.5 %collective-permute-start.4 = (bf16[2,32,640]{2,1,0:T(8,128)(2,1)}, bf16[2,32,640]{2,1,0:T(8,128)(2,1)S(1)}, u32[]{:S(2)}, u32[]{:S(2)}) collective-permute-start(bf16[2,32,640]{2,1,0:T(8,128)(2,1)} %bitcast.31), channel_id=1, source_target_pairs={{0,1},{1,0},{2,3},{3,2},{4,5},{5,4},{6,7},{7,6},{8,9},{9,8},{10,11... | collective-permute-start | bytes 245768 | tf_op jit(solution)/shard_map/ppermute | solution.py:23
  0.5 8.8 %collective-permute-start.11 = (bf16[1,2,32,640]{3,2,1,0:T(8,128)(2,1)}, bf16[1,2,32,640]{3,2,1,0:T(8,128)(2,1)S(1)}, u32[]{:S(2)}, u32[]{:S(2)}) collective-permute-start(bf16[1,2,32,640]{3,2,1,0:T(8,128)(2,1)} %bitcast.20), channel_id=1, source_target_pairs={{0,8},{1,9},{2,10},{3,11},{4,12},{5,13},{6,14},{7,15},{8,0},{9,1},... | collective-permute-start | bytes 245768 | tf_op jit(solution)/shard_map/ppermute | solution.py:23
  5.1 6.1 %collective-permute-start = (f32[4,640]{1,0:T(4,128)S(1)}, f32[4,640]{1,0:T(4,128)S(1)}, u32[]{:S(2)}, u32[]{:S(2)}) collective-permute-start(f32[4,640]{1,0:T(4,128)S(1)} %pad_maximum_fusion.3), channel_id=1, source_target_pairs={{0,8},{1,9},{2,10},{3,11},{4,12},{5,13},{6,14},{7,15},{8,0},{9,1},... | collective-permute-start | bytes 30728 | tf_op jit(solution)/shard_map/ppermute | solution.py:23
  10.2 6.0 %collective-permute-start.12 = (bf16[2,2,32,640]{3,2,1,0:T(8,128)(2,1)S(1)}, bf16[2,2,32,640]{3,2,1,0:T(8,128)(2,1)S(1)}, u32[]{:S(2)}, u32[]{:S(2)}) collective-permute-start(bf16[2,2,32,640]{3,2,1,0:T(8,128)(2,1)S(1)} %pad_maximum_fusion.2), channel_id=1, source_target_pairs={{0,4},{1,5},{2,6},{3,7},{4,0},{5,1},{6,2},{7,3},{8,12},{9,13},{10,... | collective-permute-start | bytes 491528 | tf_op jit(solution)/shard_map/ppermute | solution.py:23
  11.2 14.5 %collective-permute-start.1 = (f32[4,640]{1,0:T(4,128)S(1)}, f32[4,640]{1,0:T(4,128)S(1)}, u32[]{:S(2)}, u32[]{:S(2)}) collective-permute-start(f32[4,640]{1,0:T(4,128)S(1)} %fusion.1), channel_id=1, source_target_pairs={{0,4},{1,5},{2,6},{3,7},{4,0},{5,1},{6,2},{7,3},{8,12},{9,13},{10,... | collective-permute-start | bytes 30728 | tf_op jit(solution)/shard_map/ppermute | solution.py:23
  17.1 8.5 %collective-permute-start.13 = (bf16[4,2,32,640]{3,2,1,0:T(8,128)(2,1)S(1)}, bf16[4,2,32,640]{3,2,1,0:T(8,128)(2,1)S(1)}, u32[]{:S(2)}, u32[]{:S(2)}) collective-permute-start(bf16[4,2,32,640]{3,2,1,0:T(8,128)(2,1)S(1)} %pad_maximum_fusion.1), channel_id=1, source_target_pairs={{0,2},{1,3},{2,0},{3,1},{4,6},{5,7},{6,4},{7,5},{8,10},{9,11},{10,... | collective-permute-start | bytes 983048 | tf_op jit(solution)/shard_map/ppermute | solution.py:23
  19.5 11.3 %copy-start.3 = (bf16[2,40,640]{2,1,0:T(8,128)(2,1)}, bf16[2,40,640]{2,1,0:T(8,128)(2,1)S(1)}, u32[]{:S(2)}) copy-start(bf16[2,40,640]{2,1,0:T(8,128)(2,1)S(1)} %maximum_maximum_fusion.level_ref) | copy-start | bytes 307204
  19.5 11.3 %collective-permute-start.5 = (bf16[2,40,640]{2,1,0:T(8,128)(2,1)S(1)}, bf16[2,40,640]{2,1,0:T(8,128)(2,1)S(1)}, u32[]{:S(2)}, u32[]{:S(2)}) collective-permute-start(bf16[2,40,640]{2,1,0:T(8,128)(2,1)S(1)} %maximum_maximum_fusion.level_ref), channel_id=1, source_target_pairs={{0,2},{1,3},{2,4},{3,5},{4,6},{5,7},{6,8},{7,9},{8,10},{9,11},{10,... | collective-permute-start | bytes 307208 | tf_op jit(solution)/shard_map/ppermute | solution.py:29
  22.2 8.7 %collective-permute-start.6 = (bf16[2,40,640]{2,1,0:T(8,128)(2,1)S(1)}, bf16[2,40,640]{2,1,0:T(8,128)(2,1)S(1)}, u32[]{:S(2)}, u32[]{:S(2)}) collective-permute-start(bf16[2,40,640]{2,1,0:T(8,128)(2,1)S(1)} %maximum_maximum_fusion.level_ref), channel_id=1, source_target_pairs={{2,0},{3,1},{4,2},{5,3},{6,4},{7,5},{8,6},{9,7},{10,8},{11,9},{12,... | collective-permute-start | bytes 307208 | tf_op jit(solution)/shard_map/ppermute | solution.py:29
  25.7 31.2 %collective-permute-start.14 = (bf16[8,2,32,640]{3,2,1,0:T(8,128)(2,1)S(1)}, bf16[8,2,32,640]{3,2,1,0:T(8,128)(2,1)S(1)}, u32[]{:S(2)}, u32[]{:S(2)}) collective-permute-start(bf16[8,2,32,640]{3,2,1,0:T(8,128)(2,1)S(1)} %pad_maximum_fusion), channel_id=1, source_target_pairs={{0,1},{1,0},{2,3},{3,2},{4,5},{5,4},{6,7},{7,6},{8,9},{9,8},{10,11... | collective-permute-start | bytes 1966088 | tf_op jit(solution)/shard_map/ppermute | solution.py:23
  25.8 3.8 %collective-permute-start.2 = (f32[4,640]{1,0:T(4,128)S(1)}, f32[4,640]{1,0:T(4,128)S(1)}, u32[]{:S(2)}, u32[]{:S(2)}) collective-permute-start(f32[4,640]{1,0:T(4,128)S(1)} %add.23), channel_id=1, source_target_pairs={{0,2},{1,3},{2,0},{3,1},{4,6},{5,7},{6,4},{7,5},{8,10},{9,11},{10,... | collective-permute-start | bytes 30728 | tf_op jit(solution)/shard_map/ppermute | solution.py:23
  29.6 1.2 %copy-start.9 = (f32[4,640]{1,0:T(4,128)}, f32[4,640]{1,0:T(4,128)S(1)}, u32[]{:S(2)}) copy-start(f32[4,640]{1,0:T(4,128)S(1)} %add.24.mine_ref) | copy-start | bytes 30724
  29.6 1.2 %collective-permute-start.3 = (f32[4,640]{1,0:T(4,128)S(1)}, f32[4,640]{1,0:T(4,128)S(1)}, u32[]{:S(2)}, u32[]{:S(2)}) collective-permute-start(f32[4,640]{1,0:T(4,128)S(1)} %add.24.mine_ref), channel_id=1, source_target_pairs={{0,1},{1,0},{2,3},{3,2},{4,5},{5,4},{6,7},{7,6},{8,9},{9,8},{10,11... | collective-permute-start | bytes 30728 | tf_op jit(solution)/shard_map/ppermute | solution.py:23
  30.8 0.7 copy-start.7
  31.5 18.5 %copy-start.4 = (bf16[2,77,640]{2,0,1:T(2,128)(2,1)S(1)}, bf16[2,77,640]{2,0,1:T(2,128)(2,1)}, u32[]{:S(2)}) copy-start(bf16[2,77,640]{2,0,1:T(2,128)(2,1)} %param.34) | copy-start | bytes 591364
  31.5 19.2 %copy-start.5 = (bf16[2,77,640]{2,0,1:T(2,128)(2,1)S(1)}, bf16[2,77,640]{2,0,1:T(2,128)(2,1)}, u32[]{:S(2)}) copy-start(bf16[2,77,640]{2,0,1:T(2,128)(2,1)} %param.35) | copy-start | bytes 591364
  31.5 22.2 %copy-start = (bf16[640,640]{1,0:T(8,128)(2,1)S(1)}, bf16[640,640]{1,0:T(8,128)(2,1)}, u32[]{:S(2)}) copy-start(bf16[640,640]{1,0:T(8,128)(2,1)} %wk_ref.1) | copy-start | bytes 2457604
  37.1 8.5 %collective-permute-start.7 = (f32[4,640]{1,0:T(4,128)}, f32[4,640]{1,0:T(4,128)S(1)}, u32[]{:S(2)}, u32[]{:S(2)}) collective-permute-start(f32[4,640]{1,0:T(4,128)} %get-tuple-element.8), channel_id=1, source_target_pairs={{0,8},{1,9},{2,10},{3,11},{4,12},{5,13},{6,14},{7,15},{8,0},{9,1},... | collective-permute-start | bytes 30728 | tf_op jit(solution)/shard_map/ppermute | solution.py:23
  46.3 3.7 %collective-permute-start.8 = (f32[4,640]{1,0:T(4,128)S(1)}, f32[4,640]{1,0:T(4,128)S(1)}, u32[]{:S(2)}, u32[]{:S(2)}) collective-permute-start(f32[4,640]{1,0:T(4,128)S(1)} %add.26), channel_id=1, source_target_pairs={{0,4},{1,5},{2,6},{3,7},{4,0},{5,1},{6,2},{7,3},{8,12},{9,13},{10,... | collective-permute-start | bytes 30728 | tf_op jit(solution)/shard_map/ppermute | solution.py:23
  50.0 3.7 %collective-permute-start.9 = (f32[4,640]{1,0:T(4,128)S(1)}, f32[4,640]{1,0:T(4,128)S(1)}, u32[]{:S(2)}, u32[]{:S(2)}) collective-permute-start(f32[4,640]{1,0:T(4,128)S(1)} %add.27), channel_id=1, source_target_pairs={{0,2},{1,3},{2,0},{3,1},{4,6},{5,7},{6,4},{7,5},{8,10},{9,11},{10,... | collective-permute-start | bytes 30728 | tf_op jit(solution)/shard_map/ppermute | solution.py:23
  51.4 3.9 %copy-start.1 = (bf16[640,640]{1,0:T(8,128)(2,1)S(1)}, bf16[640,640]{1,0:T(8,128)(2,1)}, u32[]{:S(2)}) copy-start(bf16[640,640]{1,0:T(8,128)(2,1)} %wv_ref.1) | copy-start | bytes 2457604
  53.7 3.3 %copy-start.8 = (f32[4,640]{1,0:T(4,128)}, f32[4,640]{1,0:T(4,128)S(1)}, u32[]{:S(2)}) copy-start(f32[4,640]{1,0:T(4,128)S(1)} %add.28.mine_ref) | copy-start | bytes 30724
  53.7 6.5 %collective-permute-start.10 = (f32[4,640]{1,0:T(4,128)S(1)}, f32[4,640]{1,0:T(4,128)S(1)}, u32[]{:S(2)}, u32[]{:S(2)}) collective-permute-start(f32[4,640]{1,0:T(4,128)S(1)} %add.28.mine_ref), channel_id=1, source_target_pairs={{0,1},{1,0},{2,3},{3,2},{4,5},{5,4},{6,7},{7,6},{8,9},{9,8},{10,11... | collective-permute-start | bytes 30728 | tf_op jit(solution)/shard_map/ppermute | solution.py:23
  (3 other events, 1.8 us)

commit v2 on v1

--- a/solution.py
+++ b/solution.py
@@ -79,35 +79,72 @@
     )
 
 
-def conv_body(
-    features_ref, mine_ref, other_ref, gain_ref, bias_ref, above_ref, level_ref, below_ref,
-    conv_bias_ref, weight_ref, hidden_ref, sums_ref, weight_buf, sem, *, count,
-):
-    order = (0, 2, 1)
-    copies = [pltpu.make_async_copy(weight_ref.at[i], weight_buf.at[i], sem.at[i]) for i in order]
+def long_taps(middle, left, right):
+    return jnp.concatenate([t.astype(BF16) for t in three_taps(middle, left, right)], axis=1)
+
+
+def stale_body(above_ref, below_ref, weight_ref, out_ref, weight_buf, sem):
+    copies = [pltpu.make_async_copy(weight_ref.at[2 * i], weight_buf.at[i], sem.at[i]) for i in range(2)]
     for copy in copies:
         copy.start()
     images = above_ref.shape[0]
+    cells, channels = out_ref.shape
+    columns = cells // images
+    acc = None
+    for i, ref in enumerate((above_ref, below_ref)):
+        held = [ref[image].astype(F32) for image in range(images)]
+        tap = jnp.concatenate(
+            [long_taps(h[:columns], h[columns : columns + 1], h[columns + 1 : columns + 2]) for h in held],
+            axis=0,
+        )
+        copies[i].wait()
+        part = dot(tap, weight_buf[i].reshape(3 * channels, channels))
+        acc = part if acc is None else acc + part
+    out_ref[...] = acc
+
+
+def stale_conv(above, below, conv_weight, cells):
+    channels = conv_weight.shape[-1]
+    return pl.pallas_call(
+        stale_body,
+        in_specs=[VMEM, VMEM, HBM],
+        out_specs=VMEM,
+        out_shape=jax.ShapeDtypeStruct((cells, channels), F32),
+        scratch_shapes=[
+            pltpu.VMEM((2,) + conv_weight.shape[1:], BF16),
+            pltpu.SemaphoreType.DMA((2,)),
+        ],
+        cost_estimate=pl.CostEstimate(
+            flops=12 * cells * channels * channels,
+            transcendentals=0,
+            bytes_accessed=12 * channels * channels,
+        ),
+        name="stale_conv",
+    )(above, below, conv_weight)
+
+
+def conv_body(
+    features_ref, mine_ref, other_ref, gain_ref, bias_ref, level_ref, stale_ref,
+    conv_bias_ref, weight_ref, hidden_ref, sums_ref, weight_buf, sem, *, count,
+):
+    copy = pltpu.make_async_copy(weight_ref.at[1], weight_buf, sem.at[0])
+    copy.start()
+    images = level_ref.shape[0]
     cells, channels = features_ref.shape
     columns = cells // images
     moments = per_channel(mine_ref[...] + other_ref[...], count)
     gain, bias, conv_bias = [r[...].reshape(1, channels) for r in (gain_ref, bias_ref, conv_bias_ref)]
-    taps = ([], [], [])
+    taps = []
     for image in range(images):
         x = features_ref[image * columns : (image + 1) * columns].astype(F32)
         x = normalised(x, moments, image, images, gain, bias)
-        fresh = x * jax.nn.sigmoid(x)
-        for i, ref in enumerate((above_ref, level_ref, below_ref)):
-            held = ref[image].astype(F32)
-            middle = fresh if i == 1 else held[:columns]
-            edges = (held[columns : columns + 1], held[columns + 1 : columns + 2])
-            row_taps = three_taps(middle, *edges)
-            taps[i].append(jnp.concatenate([t.astype(BF16) for t in row_taps], axis=1))
-    acc = features_ref[...].astype(F32) + conv_bias
-    for i, copy in zip(order, copies):
-        copy.wait()
-        tap = jnp.concatenate(taps[i], axis=0)
-        acc = acc + dot(tap, weight_buf[i].reshape(3 * channels, channels))
+        held = level_ref[image].astype(F32)
+        taps.append(
+            long_taps(x * jax.nn.sigmoid(x), held[columns : columns + 1], held[columns + 1 : columns + 2])
+        )
+    acc = features_ref[...].astype(F32) + conv_bias + stale_ref[...]
+    copy.wait()
+    acc = acc + dot(jnp.concatenate(taps, axis=0), weight_buf[...].reshape(3 * channels, channels))
     hidden_ref[...] = acc
     for image in range(images):
         x = acc[image * columns : (image + 1) * columns]
@@ -115,27 +152,27 @@
         sums_ref[images + image : images + image + 1] = jnp.sum(x * x, axis=0, keepdims=True)
 
 
-def conv(features, sums, gain, bias, above, level, below, conv_bias, conv_weight, count):
+def conv(features, sums, gain, bias, level, stale, conv_bias, conv_weight, count):
     cells, channels = features.shape
     return pl.pallas_call(
         functools.partial(conv_body, count=count),
-        in_specs=[VMEM] * 9 + [HBM],
+        in_specs=[VMEM] * 8 + [HBM],
         out_specs=[VMEM, VMEM],
         out_shape=[
             jax.ShapeDtypeStruct((cells, channels), F32),
             jax.ShapeDtypeStruct(sums[0].shape, F32),
         ],
         scratch_shapes=[
-            pltpu.VMEM(conv_weight.shape, BF16),
-            pltpu.SemaphoreType.DMA((3,)),
+            pltpu.VMEM(conv_weight.shape[1:], BF16),
+            pltpu.SemaphoreType.DMA((1,)),
         ],
         cost_estimate=pl.CostEstimate(
-            flops=18 * cells * channels * channels,
+            flops=6 * cells * channels * channels,
             transcendentals=cells * channels,
-            bytes_accessed=18 * channels * channels,
+            bytes_accessed=6 * channels * channels,
         ),
         name="conv",
-    )(features, *sums, gain, bias, above, level, below, conv_bias, conv_weight)
+    )(features, *sums, gain, bias, level, stale, conv_bias, conv_weight)
 
 
 def attention(queries, key_of, value_of):
@@ -293,9 +330,10 @@
         for part in (held, other):
             kept.append(dot(part.reshape(-1, channels), weight).astype(BF16).reshape(part.shape))
 
+    partial = stale_conv(above, below, conv_weight, cells)
     hidden, sums = conv(
         features.reshape(cells, channels), sums, first_gain, first_bias,
-        above, level, below, conv_bias, conv_weight, count,
+        level, partial, conv_bias, conv_weight, count,
     )
     sums = total_over(sums, "patch")
     out = tail(

time: 69.2 us -> 75.2 us (1.087)
  Pallas kernels: 13.7 us -> 17.2 us
  starting transfers between devices: 22 us -> 25.3 us
  waiting for transfers between devices: 19.1 us -> 17 us
  local copies, waits for them, and re-layouts: 2.76 us -> 3.96 us
    pallas_call x0 -> x1, Pallas kernels: none -> 5.03 us  [stale_conv(): pl.pallas_call(stale_body, in_specs=[VMEM, VMEM, HBM], out_specs=VMEM, ou...]
    ppermute x13, starting transfers between devices: 18.1 us -> 21.7 us  [exchange(): lax.ppermute(value, axis, [(i, i ^ apart) for i in range(lax.axis_size(ax...]
    ppermute x13, waiting for transfers between devices: 19.1 us -> 17 us  [exchange(): lax.ppermute(value, axis, [(i, i ^ apart) for i in range(lax.axis_size(ax...]
    pallas_call x1, Pallas kernels: 5.63 us -> 4.1 us  [conv(): pl.pallas_call(functools.partial(conv_body, count=count), in_specs=[VMEM]...]
    unnamed x26, local copies, waits for them, and re-layouts: 2.68 us -> 3.88 us
  transfers between devices with their start and end apart: 15 -> 15, of which waited for: 8 -> 8; matrix products, arithmetic and copies ran while one was open for 18% -> 17% of each run, Pallas kernels for 8% -> 12%
where the time goes in v2:
time: 75.2 us; the launch traced here: 74.8 us
  starting transfers between devices  25.3 us (34%)
  Pallas kernels  17.2 us (23%)
  waiting for transfers between devices  17 us (23%)
  matrix products  6.45 us (9%)
  other arithmetic  4.6 us (6%)
  local copies, waits for them, and re-layouts  3.96 us (5%)
    ppermute x13, starting transfers between devices, exchange(): lax.ppermute(value, axis, [(i, i ^ apart) for i in range(lax.axis_size(ax...  21.7 us
    ppermute x13, waiting for transfers between devices, exchange(): lax.ppermute(value, axis, [(i, i ^ apart) for i in range(lax.axis_size(ax...  17 us
    pallas_call x1, Pallas kernels, tail(): pl.pallas_call(functools.partial(tail_body, count=count), in_specs=[VMEM]...  8.09 us
    dot_general x4, matrix products, dot(): return jnp.dot(a, b, preferred_element_type=F32)  6.45 us
    pallas_call x1, Pallas kernels, stale_conv(): pl.pallas_call(stale_body, in_specs=[VMEM, VMEM, HBM], out_specs=VMEM, ou...  5.03 us
    pallas_call x1, Pallas kernels, conv(): pl.pallas_call(functools.partial(conv_body, count=count), in_specs=[VMEM]...  4.1 us
    unnamed x26, local copies, waits for them, and re-layouts  3.88 us
    ppermute x2, starting transfers between devices, shifted(): lax.ppermute(value, axis, [(source, source + steps) for source in range(i...  3.57 us
  transfers between devices with their start and end apart: 15, of which 8 were waited for; matrix products, arithmetic and copies ran while one was open for 17% of the time, Pallas kernels for 12%

profile of v2, /device:TPU:0, one launch (start us, length us, event | category | flops | bytes accessed | tf_op | source)
XLA Modules:
  0.0 74.8 jit_solution(6240189686357932518)
XLA Ops:
  0.0 4.1 %collective-permute-start.11 = (bf16[1,2,32,640]{3,2,1,0:T(8,128)(2,1)}, bf16[1,2,32,640]{3,2,1,0:T(8,128)(2,1)S(1)}, u32[]{:S(2)}, u32[]{:S(2)}) collective-permute-start(bf16[1,2,32,640]{3,2,1,0:T(8,128)(2,1)} %bitcast.20), channel_id=1, source_target_pairs={{0,8},{1,9},{2,10},{3,11},{4,12},{5,13},{6,14},{7,15},{8,0},{9,1},... | collective-permute-start | bytes 245768 | tf_op jit(solution)/shard_map/ppermute | solution.py:23
  4.1 4.5 %collective-permute-done.11 = bf16[1,2,32,640]{3,2,1,0:T(8,128)(2,1)S(1)} collective-permute-done((bf16[1,2,32,640]{3,2,1,0:T(8,128)(2,1)}, bf16[1,2,32,640]{3,2,1,0:T(8,128)(2,1)S(1)}, u32[]{:S(2)}, u32[]{:S(2)}) %collective-permute-start.11) | collective-permute-done | bytes 81952 | tf_op jit(solution)/shard_map/ppermute | solution.py:23
  11.2 3.3 %collective-permute-start = (f32[4,640]{1,0:T(4,128)S(1)}, f32[4,640]{1,0:T(4,128)S(1)}, u32[]{:S(2)}, u32[]{:S(2)}) collective-permute-start(f32[4,640]{1,0:T(4,128)S(1)} %pad_maximum_fusion.3), channel_id=1, source_target_pairs={{0,8},{1,9},{2,10},{3,11},{4,12},{5,13},{6,14},{7,15},{8,0},{9,1},... | collective-permute-start | bytes 30728 | tf_op jit(solution)/shard_map/ppermute | solution.py:23
  15.8 1.7 %collective-permute-start.13 = (bf16[4,2,32,640]{3,2,1,0:T(8,128)(2,1)S(1)}, bf16[4,2,32,640]{3,2,1,0:T(8,128)(2,1)S(1)}, u32[]{:S(2)}, u32[]{:S(2)}) collective-permute-start(bf16[4,2,32,640]{3,2,1,0:T(8,128)(2,1)S(1)} %pad_maximum_fusion.1), channel_id=1, source_target_pairs={{0,2},{1,3},{2,0},{3,1},{4,6},{5,7},{6,4},{7,5},{8,10},{9,11},{10,... | collective-permute-start | bytes 983048 | tf_op jit(solution)/shard_map/ppermute | solution.py:23
  17.5 1.0 %maximum_maximum_fusion.level_ref = bf16[2,40,640]{2,1,0:T(8,128)(2,1)S(1)} fusion(bf16[2,1,640]{2,1,0:T(2,128)(2,1)S(1)} %get-tuple-element.12, bf16[2,1,640]{2,1,0:T(2,128)(2,1)S(1)} %get-tuple-element.11, bf16[2,32,640]{2,1,0:T(8,128)(2,1)} %bitcast.32, bf16[40]{0:T(256)(128)(2,1)S(1)} %pad.12.clone), kind=kLoop, calls=%fused_computation.10 | loop fusion | flops 409600 | bytes 189520 | tf_op jit(solution)/shard_map/concatenate | solution.py:317
  18.5 2.3 %collective-permute-start.5 = (bf16[2,40,640]{2,1,0:T(8,128)(2,1)S(1)}, bf16[2,40,640]{2,1,0:T(8,128)(2,1)S(1)}, u32[]{:S(2)}, u32[]{:S(2)}) collective-permute-start(bf16[2,40,640]{2,1,0:T(8,128)(2,1)S(1)} %maximum_maximum_fusion.level_ref), channel_id=1, source_target_pairs={{0,2},{1,3},{2,4},{3,5},{4,6},{5,7},{6,8},{7,9},{8,10},{9,11},{10,... | collective-permute-start | bytes 307208 | tf_op jit(solution)/shard_map/ppermute | solution.py:29
  20.8 1.3 %collective-permute-start.6 = (bf16[2,40,640]{2,1,0:T(8,128)(2,1)S(1)}, bf16[2,40,640]{2,1,0:T(8,128)(2,1)S(1)}, u32[]{:S(2)}, u32[]{:S(2)}) collective-permute-start(bf16[2,40,640]{2,1,0:T(8,128)(2,1)S(1)} %maximum_maximum_fusion.level_ref), channel_id=1, source_target_pairs={{2,0},{3,1},{4,2},{5,3},{6,4},{7,5},{8,6},{9,7},{10,8},{11,9},{12,... | collective-permute-start | bytes 307208 | tf_op jit(solution)/shard_map/ppermute | solution.py:29
  22.1 2.7 %collective-permute-done.13 = bf16[4,2,32,640]{3,2,1,0:T(8,128)(2,1)S(1)} collective-permute-done((bf16[4,2,32,640]{3,2,1,0:T(8,128)(2,1)S(1)}, bf16[4,2,32,640]{3,2,1,0:T(8,128)(2,1)S(1)}, u32[]{:S(2)}, u32[]{:S(2)}) %collective-permute-start.13) | collective-permute-done | bytes 327712 | tf_op jit(solution)/shard_map/ppermute | solution.py:23
  25.0 4.0 %collective-permute-start.1 = (f32[4,640]{1,0:T(4,128)S(1)}, f32[4,640]{1,0:T(4,128)S(1)}, u32[]{:S(2)}, u32[]{:S(2)}) collective-permute-start(f32[4,640]{1,0:T(4,128)S(1)} %fusion.1), channel_id=1, source_target_pairs={{0,4},{1,5},{2,6},{3,7},{4,0},{5,1},{6,2},{7,3},{8,12},{9,13},{10,... | collective-permute-start | bytes 30728 | tf_op jit(solution)/shard_map/ppermute | solution.py:23
  29.0 1.7 %collective-permute-done.1 = f32[4,640]{1,0:T(4,128)S(1)} collective-permute-done((f32[4,640]{1,0:T(4,128)S(1)}, f32[4,640]{1,0:T(4,128)S(1)}, u32[]{:S(2)}, u32[]{:S(2)}) %collective-permute-start.1) | collective-permute-done | bytes 10272 | tf_op jit(solution)/shard_map/ppermute | solution.py:23
  30.7 1.5 %collective-permute-start.2 = (f32[4,640]{1,0:T(4,128)S(1)}, f32[4,640]{1,0:T(4,128)S(1)}, u32[]{:S(2)}, u32[]{:S(2)}) collective-permute-start(f32[4,640]{1,0:T(4,128)S(1)} %add.23), channel_id=1, source_target_pairs={{0,2},{1,3},{2,0},{3,1},{4,6},{5,7},{6,4},{7,5},{8,10},{9,11},{10,... | collective-permute-start | bytes 30728 | tf_op jit(solution)/shard_map/ppermute | solution.py:23
  32.2 2.1 %collective-permute-done.2 = f32[4,640]{1,0:T(4,128)S(1)} collective-permute-done((f32[4,640]{1,0:T(4,128)S(1)}, f32[4,640]{1,0:T(4,128)S(1)}, u32[]{:S(2)}, u32[]{:S(2)}) %collective-permute-start.2) | collective-permute-done | bytes 10272 | tf_op jit(solution)/shard_map/ppermute | solution.py:23
  35.7 5.0 %stale_conv.1.stale_ref = f32[64,640]{1,0:T(8,128)} custom-call(bf16[2,40,640]{2,1,0:T(8,128)(2,1)} %copy-done.6, bf16[2,40,640]{2,1,0:T(8,128)(2,1)} %copy-done.7, bf16[3,3,640,640]{3,2,1,0:T(8,128)(2,1)} %weight_ref.3), custom_call_target="tpu_custom_call" | custom-call | flops 314572800 | bytes 4915200 | tf_op jit(solution)/shard_map/stale_conv/pallas_call | solution.py:108
  41.3 4.1 %conv.1 = (f32[64,640]{1,0:T(8,128)}, f32[4,640]{1,0:T(4,128)}) custom-call(bf16[64,640]{1,0:T(8,128)(2,1)} %bitcast.30, f32[4,640]{1,0:T(4,128)} %copy-done.9, f32[4,640]{1,0:T(4,128)} %copy-done.11, f32[640]{0:T(1024)} %gain_ref.2, f32[640]{0:T(1024)} %bias_ref.2, bf16[2,40,640]{2,1,0:T(8,128)(2,1)} %copy-done.3, f32[64,640]{1,0:T(8,128)} %stale_conv.1.stale_ref, ...), custom_call_target="tpu_custom_call" | custom-call | flops 157286400 | bytes 2457600 | tf_op jit(solution)/shard_map/conv/pallas_call | solution.py:157
  45.4 4.2 %collective-permute-start.7 = (f32[4,640]{1,0:T(4,128)}, f32[4,640]{1,0:T(4,128)S(1)}, u32[]{:S(2)}, u32[]{:S(2)}) collective-permute-start(f32[4,640]{1,0:T(4,128)} %get-tuple-element.8), channel_id=1, source_target_pairs={{0,8},{1,9},{2,10},{3,11},{4,12},{5,13},{6,14},{7,15},{8,0},{9,1},... | collective-permute-start | bytes 30728 | tf_op jit(solution)/shard_map/ppermute | solution.py:23
  49.7 1.9 %collective-permute-done.7 = f32[4,640]{1,0:T(4,128)S(1)} collective-permute-done((f32[4,640]{1,0:T(4,128)}, f32[4,640]{1,0:T(4,128)S(1)}, u32[]{:S(2)}, u32[]{:S(2)}) %collective-permute-start.7) | collective-permute-done | bytes 10272 | tf_op jit(solution)/shard_map/ppermute | solution.py:23
  52.2 1.6 %collective-permute-start.8 = (f32[4,640]{1,0:T(4,128)S(1)}, f32[4,640]{1,0:T(4,128)S(1)}, u32[]{:S(2)}, u32[]{:S(2)}) collective-permute-start(f32[4,640]{1,0:T(4,128)S(1)} %add.26), channel_id=1, source_target_pairs={{0,4},{1,5},{2,6},{3,7},{4,0},{5,1},{6,2},{7,3},{8,12},{9,13},{10,... | collective-permute-start | bytes 30728 | tf_op jit(solution)/shard_map/ppermute | solution.py:23
  53.9 2.0 %collective-permute-done.8 = f32[4,640]{1,0:T(4,128)S(1)} collective-permute-done((f32[4,640]{1,0:T(4,128)S(1)}, f32[4,640]{1,0:T(4,128)S(1)}, u32[]{:S(2)}, u32[]{:S(2)}) %collective-permute-start.8) | collective-permute-done | bytes 10272 | tf_op jit(solution)/shard_map/ppermute | solution.py:23
  57.6 1.9 %collective-permute-done.9 = f32[4,640]{1,0:T(4,128)S(1)} collective-permute-done((f32[4,640]{1,0:T(4,128)S(1)}, f32[4,640]{1,0:T(4,128)S(1)}, u32[]{:S(2)}, u32[]{:S(2)}) %collective-permute-start.9) | collective-permute-done | bytes 10272 | tf_op jit(solution)/shard_map/ppermute | solution.py:23
  59.6 1.6 %convolution_convert_fusion.3 = bf16[512,640]{1,0:T(8,128)(2,1)} fusion(bf16[512,640]{1,0:T(8,128)(2,1)S(1)} %bitcast.28, bf16[640,640]{1,0:T(8,128)(2,1)S(1)} %copy-done), kind=kOutput, calls=%fused_computation.3 | convolution fusion | flops 419758080 | bytes 2129920 | tf_op jit(solution)/shard_map/dot_general | solution.py:43
  61.2 1.6 %convolution_convert_fusion.1 = bf16[512,640]{1,0:T(8,128)(2,1)} fusion(bf16[512,640]{1,0:T(8,128)(2,1)S(1)} %bitcast.29, bf16[640,640]{1,0:T(8,128)(2,1)S(1)} %copy-done.1), kind=kOutput, calls=%fused_computation.1 | convolution fusion | flops 419758080 | bytes 2129920 | tf_op jit(solution)/shard_map/dot_general | solution.py:43
  62.9 1.6 %convolution_convert_fusion.2 = bf16[512,640]{1,0:T(8,128)(2,1)} fusion(bf16[512,640]{1,0:T(8,128)(2,1)S(1)} %bitcast.33, bf16[640,640]{1,0:T(8,128)(2,1)S(1)} %copy-done), kind=kOutput, calls=%fused_computation.2 | convolution fusion | flops 419758080 | bytes 2129920 | tf_op jit(solution)/shard_map/dot_general | solution.py:43
  64.5 1.6 %convolution_convert_fusion = bf16[512,640]{1,0:T(8,128)(2,1)} fusion(bf16[512,640]{1,0:T(8,128)(2,1)S(1)} %bitcast.34, bf16[640,640]{1,0:T(8,128)(2,1)S(1)} %copy-done.1), kind=kOutput, calls=%fused_computation | convolution fusion | flops 419758080 | bytes 2129920 | tf_op jit(solution)/shard_map/dot_general | solution.py:43
  66.7 8.1 %tail.1 = f32[64,640]{1,0:T(8,128)} custom-call(f32[64,640]{1,0:T(8,128)} %get-tuple-element.7.hidden_ref, f32[4,640]{1,0:T(4,128)} %copy-done.8, f32[4,640]{1,0:T(4,128)} %copy-done.10, f32[640]{0:T(1024)} %gain_ref.3, f32[640]{0:T(1024)} %bias_ref.3, f32[640]{0:T(1024)} %layer_gain_ref.1, bf16[2,77,640]{2,1,0:T(8,128)(2,1)} %copy.19.text_keys_ref, ...), custom_call_target="tpu_custom_call" | custom-call | flops 482344960 | bytes 7536640 | tf_op jit(solution)/shard_map/tail/pallas_call | solution.py:279
  (54 shorter events, 9.0 us)
Async XLA Ops:
  0.0 24.8 %copy-start.2 = (bf16[2,1,32,640]{3,2,1,0:T(8,128)(2,1)S(1)}, bf16[2,1,32,640]{3,2,1,0:T(8,128)(2,1)}, u32[]{:S(2)}) copy-start(bf16[2,1,32,640]{3,2,1,0:T(8,128)(2,1)} %param.20) | copy-start | bytes 245764
  0.0 8.5 %collective-permute-start.11 = (bf16[1,2,32,640]{3,2,1,0:T(8,128)(2,1)}, bf16[1,2,32,640]{3,2,1,0:T(8,128)(2,1)S(1)}, u32[]{:S(2)}, u32[]{:S(2)}) collective-permute-start(bf16[1,2,32,640]{3,2,1,0:T(8,128)(2,1)} %bitcast.20), channel_id=1, source_target_pairs={{0,8},{1,9},{2,10},{3,11},{4,12},{5,13},{6,14},{7,15},{8,0},{9,1},... | collective-permute-start | bytes 245768 | tf_op jit(solution)/shard_map/ppermute | solution.py:23
  4.1 13.4 %collective-permute-start.4 = (bf16[2,32,640]{2,1,0:T(8,128)(2,1)}, bf16[2,32,640]{2,1,0:T(8,128)(2,1)S(1)}, u32[]{:S(2)}, u32[]{:S(2)}) collective-permute-start(bf16[2,32,640]{2,1,0:T(8,128)(2,1)} %bitcast.31), channel_id=1, source_target_pairs={{0,1},{1,0},{2,3},{3,2},{4,5},{5,4},{6,7},{7,6},{8,9},{9,8},{10,11... | collective-permute-start | bytes 245768 | tf_op jit(solution)/shard_map/ppermute | solution.py:23
  9.5 5.4 %collective-permute-start.12 = (bf16[2,2,32,640]{3,2,1,0:T(8,128)(2,1)S(1)}, bf16[2,2,32,640]{3,2,1,0:T(8,128)(2,1)S(1)}, u32[]{:S(2)}, u32[]{:S(2)}) collective-permute-start(bf16[2,2,32,640]{3,2,1,0:T(8,128)(2,1)S(1)} %pad_maximum_fusion.2), channel_id=1, source_target_pairs={{0,4},{1,5},{2,6},{3,7},{4,0},{5,1},{6,2},{7,3},{8,12},{9,13},{10,... | collective-permute-start | bytes 491528 | tf_op jit(solution)/shard_map/ppermute | solution.py:23
  11.2 13.7 %collective-permute-start = (f32[4,640]{1,0:T(4,128)S(1)}, f32[4,640]{1,0:T(4,128)S(1)}, u32[]{:S(2)}, u32[]{:S(2)}) collective-permute-start(f32[4,640]{1,0:T(4,128)S(1)} %pad_maximum_fusion.3), channel_id=1, source_target_pairs={{0,8},{1,9},{2,10},{3,11},{4,12},{5,13},{6,14},{7,15},{8,0},{9,1},... | collective-permute-start | bytes 30728 | tf_op jit(solution)/shard_map/ppermute | solution.py:23
  15.8 9.0 %collective-permute-start.13 = (bf16[4,2,32,640]{3,2,1,0:T(8,128)(2,1)S(1)}, bf16[4,2,32,640]{3,2,1,0:T(8,128)(2,1)S(1)}, u32[]{:S(2)}, u32[]{:S(2)}) collective-permute-start(bf16[4,2,32,640]{3,2,1,0:T(8,128)(2,1)S(1)} %pad_maximum_fusion.1), channel_id=1, source_target_pairs={{0,2},{1,3},{2,0},{3,1},{4,6},{5,7},{6,4},{7,5},{8,10},{9,11},{10,... | collective-permute-start | bytes 983048 | tf_op jit(solution)/shard_map/ppermute | solution.py:23
  18.5 22.2 %copy-start.3 = (bf16[2,40,640]{2,1,0:T(8,128)(2,1)}, bf16[2,40,640]{2,1,0:T(8,128)(2,1)S(1)}, u32[]{:S(2)}) copy-start(bf16[2,40,640]{2,1,0:T(8,128)(2,1)S(1)} %maximum_maximum_fusion.level_ref) | copy-start | bytes 307204
  18.5 15.9 %collective-permute-start.5 = (bf16[2,40,640]{2,1,0:T(8,128)(2,1)S(1)}, bf16[2,40,640]{2,1,0:T(8,128)(2,1)S(1)}, u32[]{:S(2)}, u32[]{:S(2)}) collective-permute-start(bf16[2,40,640]{2,1,0:T(8,128)(2,1)S(1)} %maximum_maximum_fusion.level_ref), channel_id=1, source_target_pairs={{0,2},{1,3},{2,4},{3,5},{4,6},{5,7},{6,8},{7,9},{8,10},{9,11},{10,... | collective-permute-start | bytes 307208 | tf_op jit(solution)/shard_map/ppermute | solution.py:29
  20.8 13.6 %collective-permute-start.6 = (bf16[2,40,640]{2,1,0:T(8,128)(2,1)S(1)}, bf16[2,40,640]{2,1,0:T(8,128)(2,1)S(1)}, u32[]{:S(2)}, u32[]{:S(2)}) collective-permute-start(bf16[2,40,640]{2,1,0:T(8,128)(2,1)S(1)} %maximum_maximum_fusion.level_ref), channel_id=1, source_target_pairs={{2,0},{3,1},{4,2},{5,3},{6,4},{7,5},{8,6},{9,7},{10,8},{11,9},{12,... | collective-permute-start | bytes 307208 | tf_op jit(solution)/shard_map/ppermute | solution.py:29
  24.9 38.0 %collective-permute-start.14 = (bf16[8,2,32,640]{3,2,1,0:T(8,128)(2,1)S(1)}, bf16[8,2,32,640]{3,2,1,0:T(8,128)(2,1)S(1)}, u32[]{:S(2)}, u32[]{:S(2)}) collective-permute-start(bf16[8,2,32,640]{3,2,1,0:T(8,128)(2,1)S(1)} %pad_maximum_fusion), channel_id=1, source_target_pairs={{0,1},{1,0},{2,3},{3,2},{4,5},{5,4},{6,7},{7,6},{8,9},{9,8},{10,11... | collective-permute-start | bytes 1966088 | tf_op jit(solution)/shard_map/ppermute | solution.py:23
  25.0 5.7 %collective-permute-start.1 = (f32[4,640]{1,0:T(4,128)S(1)}, f32[4,640]{1,0:T(4,128)S(1)}, u32[]{:S(2)}, u32[]{:S(2)}) collective-permute-start(f32[4,640]{1,0:T(4,128)S(1)} %fusion.1), channel_id=1, source_target_pairs={{0,4},{1,5},{2,6},{3,7},{4,0},{5,1},{6,2},{7,3},{8,12},{9,13},{10,... | collective-permute-start | bytes 30728 | tf_op jit(solution)/shard_map/ppermute | solution.py:23
  30.7 3.7 %collective-permute-start.2 = (f32[4,640]{1,0:T(4,128)S(1)}, f32[4,640]{1,0:T(4,128)S(1)}, u32[]{:S(2)}, u32[]{:S(2)}) collective-permute-start(f32[4,640]{1,0:T(4,128)S(1)} %add.23), channel_id=1, source_target_pairs={{0,2},{1,3},{2,0},{3,1},{4,6},{5,7},{6,4},{7,5},{8,10},{9,11},{10,... | collective-permute-start | bytes 30728 | tf_op jit(solution)/shard_map/ppermute | solution.py:23
  34.4 6.4 %copy-start.9 = (f32[4,640]{1,0:T(4,128)}, f32[4,640]{1,0:T(4,128)S(1)}, u32[]{:S(2)}) copy-start(f32[4,640]{1,0:T(4,128)S(1)} %add.24.mine_ref) | copy-start | bytes 30724
  34.4 6.4 %collective-permute-start.3 = (f32[4,640]{1,0:T(4,128)S(1)}, f32[4,640]{1,0:T(4,128)S(1)}, u32[]{:S(2)}, u32[]{:S(2)}) collective-permute-start(f32[4,640]{1,0:T(4,128)S(1)} %add.24.mine_ref), channel_id=1, source_target_pairs={{0,1},{1,0},{2,3},{3,2},{4,5},{5,4},{6,7},{7,6},{8,9},{9,8},{10,11... | collective-permute-start | bytes 30728 | tf_op jit(solution)/shard_map/ppermute | solution.py:23
  35.0 0.6 copy-start.7
  41.3 14.9 %copy-start.4 = (bf16[2,77,640]{2,0,1:T(2,128)(2,1)S(1)}, bf16[2,77,640]{2,0,1:T(2,128)(2,1)}, u32[]{:S(2)}) copy-start(bf16[2,77,640]{2,0,1:T(2,128)(2,1)} %param.34) | copy-start | bytes 591364
  41.3 15.6 %copy-start.5 = (bf16[2,77,640]{2,0,1:T(2,128)(2,1)S(1)}, bf16[2,77,640]{2,0,1:T(2,128)(2,1)}, u32[]{:S(2)}) copy-start(bf16[2,77,640]{2,0,1:T(2,128)(2,1)} %param.35) | copy-start | bytes 591364
  41.3 18.3 %copy-start = (bf16[640,640]{1,0:T(8,128)(2,1)S(1)}, bf16[640,640]{1,0:T(8,128)(2,1)}, u32[]{:S(2)}) copy-start(bf16[640,640]{1,0:T(8,128)(2,1)} %wk_ref.1) | copy-start | bytes 2457604
  45.4 6.1 %collective-permute-start.7 = (f32[4,640]{1,0:T(4,128)}, f32[4,640]{1,0:T(4,128)S(1)}, u32[]{:S(2)}, u32[]{:S(2)}) collective-permute-start(f32[4,640]{1,0:T(4,128)} %get-tuple-element.8), channel_id=1, source_target_pairs={{0,8},{1,9},{2,10},{3,11},{4,12},{5,13},{6,14},{7,15},{8,0},{9,1},... | collective-permute-start | bytes 30728 | tf_op jit(solution)/shard_map/ppermute | solution.py:23
  52.2 3.7 %collective-permute-start.8 = (f32[4,640]{1,0:T(4,128)S(1)}, f32[4,640]{1,0:T(4,128)S(1)}, u32[]{:S(2)}, u32[]{:S(2)}) collective-permute-start(f32[4,640]{1,0:T(4,128)S(1)} %add.26), channel_id=1, source_target_pairs={{0,4},{1,5},{2,6},{3,7},{4,0},{5,1},{6,2},{7,3},{8,12},{9,13},{10,... | collective-permute-start | bytes 30728 | tf_op jit(solution)/shard_map/ppermute | solution.py:23
  55.9 3.7 %collective-permute-start.9 = (f32[4,640]{1,0:T(4,128)S(1)}, f32[4,640]{1,0:T(4,128)S(1)}, u32[]{:S(2)}, u32[]{:S(2)}) collective-permute-start(f32[4,640]{1,0:T(4,128)S(1)} %add.27), channel_id=1, source_target_pairs={{0,2},{1,3},{2,0},{3,1},{4,6},{5,7},{6,4},{7,5},{8,10},{9,11},{10,... | collective-permute-start | bytes 30728 | tf_op jit(solution)/shard_map/ppermute | solution.py:23
  57.6 3.6 %copy-start.1 = (bf16[640,640]{1,0:T(8,128)(2,1)S(1)}, bf16[640,640]{1,0:T(8,128)(2,1)}, u32[]{:S(2)}) copy-start(bf16[640,640]{1,0:T(8,128)(2,1)} %wv_ref.1) | copy-start | bytes 2457604
  59.6 3.3 %copy-start.8 = (f32[4,640]{1,0:T(4,128)}, f32[4,640]{1,0:T(4,128)S(1)}, u32[]{:S(2)}) copy-start(f32[4,640]{1,0:T(4,128)S(1)} %add.28.mine_ref) | copy-start | bytes 30724
  59.6 6.5 %collective-permute-start.10 = (f32[4,640]{1,0:T(4,128)S(1)}, f32[4,640]{1,0:T(4,128)S(1)}, u32[]{:S(2)}, u32[]{:S(2)}) collective-permute-start(f32[4,640]{1,0:T(4,128)S(1)} %add.28.mine_ref), channel_id=1, source_target_pairs={{0,1},{1,0},{2,3},{3,2},{4,5},{5,4},{6,7},{7,6},{8,9},{9,8},{10,11... | collective-permute-start | bytes 30728 | tf_op jit(solution)/shard_map/ppermute | solution.py:23
  (3 other events, 1.8 us)
